TPU v7x, 512 devices: a whole 4x8x8 slice. The times are simulated.
512 devices in a mesh: seq: 64 (over y, x, core), chan: 8 (over z).
Axes of the slice: x: 4, y: 8, z: 8, core: 2. Of those that a mesh axis runs over, the one named last changes fastest.
Arguments:
- x_in: bfloat16 [131072, 2048], P('seq', 'chan'), may hold values from -6 to 6
- gate_in: bfloat16 [131072, 2048], P('seq', 'chan'), may hold values from -70 to 70
- b_in: bfloat16 [131072, 64], P('seq'), may hold values from -0.75 to 0.75
- c_in: bfloat16 [131072, 64], P('seq'), may hold values from -6 to 6
- step_size: float32 [32, 131072], P('chan', 'seq'), may hold values from 0 to 1, as said below
- log_keep: float32 [32, 131072], P('chan', 'seq'), may hold values from -2 to 0
- skip_gain: float32 [32], P('chan'), may hold values from 0.5 to 1.5
- norm_gain: float32 [2048], P('chan'), may hold values from 0.25 to 1.75
Outputs:
- mixed: bfloat16 [131072, 2048], P('seq', 'chan')
Inputs may be any that keep to these rules, and one draw needn't show every extreme that they name: `step_size`: positive.
All inputs are finite; a program needn't handle non-finite values.
Results may differ from a plain program's by a relative error of at most 0.005.
Values sent between devices are 32-bit elements; how exact they have to be, the bound alone decides.
No kernel may reach another device: no remote copies, remote signals or barrier semaphores. Data moves between devices by JAX's collectives and lax.ppermute only.
A program may use at most 64 MiB of HBM per device.

v0:
```python
import jax
import jax.numpy as jnp
from jax import lax
from jax.sharding import Mesh
from jax.sharding import PartitionSpec as P

CH = 2048
BLOCK = 256
SEQ = ("seq_0", "seq_1", "seq_2")


epsilon = 1e-05


def nothing_yet(shard, identity):
    return jax.tree.map(
        lambda part, zero: jnp.zeros_like(part) + jnp.asarray(zero, part.dtype), shard, identity
    )


def all_in_one(shard, axis):
    leaves = jax.tree.leaves(shard)
    order = sorted(range(len(leaves)), key=lambda k: -leaves[k].size)
    width = (1, *leaves[order[0]].shape)[-1]
    lines = [
        jnp.pad(leaves[k].reshape(-1), (0, -leaves[k].size % width)).reshape(-1, width)
        for k in order
    ]
    both, at, found = (lax.all_gather(jnp.concatenate(lines), axis), 0, {})
    for k, line in zip(order, lines):
        piece = both[:, at : at + len(line)].reshape(len(both), -1)
        found[k] = piece[:, : leaves[k].size].reshape(-1, *leaves[k].shape)
        at += len(line)
    numbers = iter(range(len(leaves)))
    return jax.tree.map(lambda _: found[next(numbers)], shard)


def prefix_by_axis(shard, axes, combine, identity):
    before = start = nothing_yet(shard, identity)
    total = shard
    for axis in reversed(axes):
        length, here = (lax.axis_size(axis), lax.axis_index(axis))
        pieces = all_in_one(total, axis)
        inside, total = (start, start)
        for k in range(length):
            passed = k < here
            total = combine(total, jax.tree.map(lambda part: part[k], pieces))
            inside = jax.tree.map(lambda new, old: jnp.where(passed, new, old), total, inside)
        before = combine(inside, before)
    return before


def copy_for_each(shard, axis):
    length = lax.axis_size(axis)
    return lax.all_to_all(
        jnp.broadcast_to(shard[None], (length, *shard.shape)), axis, 0, 0, tiled=True
    )


def of_everyone(shard, axis):
    return copy_for_each(shard, axis).sum(axis=0)


def compose(earlier, later_pair):
    early_total, early_state = earlier
    late_total, late_state = later_pair
    return (early_total + late_total, jnp.exp(late_total)[:, None] * early_state + late_state)


def incoming_state(device_total, end_flat):
    head_count, flat_size = end_flat.shape
    zeros_pair = (
        jnp.zeros((head_count,), jnp.float32),
        jnp.zeros((head_count, flat_size), jnp.float32),
    )
    _, entering = prefix_by_axis((device_total, end_flat), SEQ, compose, zeros_pair)
    return entering


def apply_state(c_blocks, cum_keep, states):
    state_high = states.astype(jnp.bfloat16)
    state_low = (states - state_high.astype(jnp.float32)).astype(jnp.bfloat16)
    projected = jnp.einsum(
        "btn,bhpn->bthp", c_blocks, state_high, preferred_element_type=jnp.float32
    )
    projected = projected + jnp.einsum(
        "btn,bhpn->bthp", c_blocks, state_low, preferred_element_type=jnp.float32
    )
    return jnp.exp(cum_keep).transpose(1, 2, 0)[:, :, :, None] * projected


def per_device(x_in, gate_in, b_in, c_in, step_size, log_keep, skip_gain, norm_gain):
    tokens, channels = x_in.shape
    head_count = step_size.shape[0]
    head_width = channels // head_count
    nstate = b_in.shape[1]
    block_count = tokens // BLOCK
    x_blocks = x_in.reshape(block_count, BLOCK, head_count, head_width)
    b_blocks = b_in.reshape(block_count, BLOCK, nstate)
    c_blocks = c_in.reshape(block_count, BLOCK, nstate)
    step_blocks = step_size.reshape(head_count, block_count, BLOCK)
    cum_keep = jnp.cumsum(log_keep.reshape(head_count, block_count, BLOCK), axis=2)
    block_total = cum_keep[:, :, -1]
    decayed_b = (
        (jnp.exp(block_total[:, :, None] - cum_keep) * step_blocks)[:, :, :, None]
        * b_blocks[None].astype(jnp.float32)
    ).astype(jnp.bfloat16)
    block_state = jnp.einsum(
        "bshp,hbsn->bhpn", x_blocks, decayed_b, preferred_element_type=jnp.float32
    )

    def carry_blocks(running, block_input):
        total_now, state_now = block_input
        return (jnp.exp(total_now)[:, None, None] * running + state_now, running)

    end_state, starts = lax.scan(
        carry_blocks,
        jnp.zeros((head_count, head_width, nstate), jnp.float32),
        (block_total.T, block_state),
    )
    device_total = jnp.sum(block_total, axis=1)
    prefix_total = jnp.cumsum(block_total, axis=1) - block_total
    end_flat = end_state.reshape(head_count, head_width * nstate)
    scores = jnp.einsum("btn,bsn->bts", c_blocks, b_blocks, preferred_element_type=jnp.float32)
    row_index = lax.broadcasted_iota(jnp.int32, (BLOCK, BLOCK), 0)
    col_index = lax.broadcasted_iota(jnp.int32, (BLOCK, BLOCK), 1)
    causal = (row_index >= col_index)[None, None]
    log_gaps = cum_keep[:, :, :, None] - cum_keep[:, :, None, :]
    decays = jnp.where(causal, jnp.exp(jnp.where(causal, log_gaps, 0.0)), 0.0)
    weights = (scores[None] * decays * step_blocks[:, :, None, :]).astype(jnp.bfloat16)
    output = jnp.einsum(
        "hbts,bshp->bthp", weights, x_blocks, preferred_element_type=jnp.float32
    ) + apply_state(c_blocks, cum_keep, starts)
    entering = incoming_state(device_total, end_flat).reshape(head_count, head_width, nstate)
    spread_state = jnp.broadcast_to(entering[None], (block_count, head_count, head_width, nstate))
    output = output + apply_state(c_blocks, cum_keep + prefix_total[:, :, None], spread_state)
    output = output + skip_gain[None, None, :, None] * x_blocks.astype(jnp.float32)
    output = output.reshape(tokens, channels)
    gated_out = output * jax.nn.silu(gate_in.astype(jnp.float32))
    squares = jnp.sum(gated_out * gated_out, axis=1)
    summed = of_everyone(squares, "chan")
    row_factor = lax.rsqrt(summed / CH + epsilon)
    return (gated_out * row_factor[:, None] * norm_gain[None, :]).astype(jnp.bfloat16)


def solution(mesh):
    split = Mesh(
        mesh.devices.reshape(8, 4, 2, mesh.shape["chan"]), ("seq_0", "seq_1", "seq_2", "chan")
    )
    placed = (
        P(SEQ, "chan"),
        P(SEQ, "chan"),
        P(SEQ, None),
        P(SEQ, None),
        P("chan", SEQ),
        P("chan", SEQ),
        P("chan"),
        P("chan"),
    )
    return jax.shard_map(
        per_device, mesh=split, in_specs=placed, out_specs=P(SEQ, "chan"), check_vma=False
    )
```

profile of v0, /device:TPU:2, one launch (start us, length us, event | category | flops | bytes accessed | tf_op | source)
XLA Modules:
  0.0 119.7 jit_solution(18137246634973519460)
XLA Ops:
  0.0 0.8 reshape.487
  0.8 2.3 %reduce-window.6 = f32[4,8,2,128]{3,1,2,0:T(8,128)S(1)} reduce-window(f32[4,8,2,128]{3,1,2,0:T(8,128)S(1)} %copy.139, f32[]{:T(128)} %constant.23.clone.1), window={size=1x1x1x128 pad=0_0x0_0x0_0x127_0}, to_apply=%region_0.0 | reduce-window | flops 1040384 | bytes 65540 | tf_op jit(solution)/shard_map/reduce-window
  3.3 0.7 exponential_bitcast_fusion.1
  4.3 1.5 %exponential_bitcast_fusion = (f32[8,256,4]{1,0,2:T(8,128)}, f32[4,8,256]{2,1,0:T(8,128)S(1)}) fusion(f32[4,8,256]{2,1,0:T(8,128)S(1)} %get-tuple-element.97, f32[4,8]{1,0:T(4,128)S(1)} %get-tuple-element.83, f32[1,4,8,256]{3,1,2,0:T(4,128)} %bitcast.180, f32[4,8]{1,0:T(4,128)S(1)} %get-tuple-element.84), kind=kLoop, calls=%fused_computation.70 | loop fusion | flops 24576 | bytes 131328 | tf_op jit(solution)/shard_map/transpose | solution.py:89
  5.8 0.6 copy.148
  6.4 3.3 %reshape.514 = bf16[8,256,4,64]{3,2,1,0:T(4,128)(2,1)S(1)} reshape(bf16[2048,256]{1,0:T(8,128)(2,1)} %param.10) | data formatting | bytes 2097152 | tf_op jit(solution)/shard_map/reshape | solution.py:98
  9.7 1.0 copy.146
  10.9 1.0 copy.149
  12.0 2.4 %convolution_bitcast_fusion = f32[8,4,64,64]{2,3,1,0:T(8,128)} fusion(bf16[8,256,4,64]{1,3,2,0:T(8,128)(2,1)S(1)} %copy.146, f32[8,256,64]{1,2,0:T(8,128)} %copy.149, f32[4,8,256]{2,0,1:T(4,128)S(1)} %copy-done.20), kind=kOutput, calls=%fused_computation.28 | convolution fusion | flops 68157440 | bytes 2129920 | tf_op jit(solution)/shard_map/bshp,hbsn->bhpn/dot_general | solution.py:108
  14.4 9.3 %while.13 = (s32[]{:T(128)}, f32[4,64,64]{2,1,0:T(8,128)S(1)}, f32[8,4,64,64]{3,2,1,0:T(8,128)S(1)}, f32[8,4]{1,0:T(8,128)S(1)}, f32[8,4,64,64]{2,3,1,0:T(8,128)}, /*index=5*/s32[]{:T(128)}, s32[]{:T(128)}) while((s32[]{:T(128)}, f32[4,64,64]{2,1,0:T(8,128)S(1)}, f32[8,4,64,64]{3,2,1,0:T(8,128)S(1)}, f32[8,4]{1,0:T(8,128)S(1)}, ...), condition=%wide.region_3.4_spmd.clone, body=%wide.region_2.3_spmd.clone.sunk | while | flops 65539 | bytes 721044 | solution.py:116
  14.5 0.9 constant_dynamic-slice_fusion.3
  15.6 0.9 constant_dynamic-slice_fusion.3
  16.8 0.9 constant_dynamic-slice_fusion.3
  18.0 0.9 constant_dynamic-slice_fusion.3
  19.1 0.9 constant_dynamic-slice_fusion.3
  20.3 0.9 constant_dynamic-slice_fusion.3
  21.5 0.9 constant_dynamic-slice_fusion.3
  22.6 0.9 constant_dynamic-slice_fusion.3
  23.9 2.0 %all-gather.3 = f32[2,5,4096]{2,1,0:T(8,128)S(1)} all-gather(f32[1,5,4096]{2,1,0:T(8,128)S(1)} %maximum_bitcast_fusion), channel_id=2, replica_groups=mesh['seq_0'=8,'seq_1'=4,'seq_2'=2,'chan'=8] {'seq_2'}, dimensions={0}, use_global_device_ids=true | all-gather | bytes 245760 | tf_op jit(solution)/shard_map/all_gather | solution.py:29
  26.2 15.8 %all-gather.4 = f32[4,5,4096]{2,1,0:T(8,128)S(1)} all-gather(f32[1,5,4096]{2,1,0:T(8,128)S(1)} %maximum_bitcast_fusion.1), channel_id=3, replica_groups=mesh['seq_0'=8,'seq_1'=4,'seq_2'=2,'chan'=8] {'seq_1'}, dimensions={0}, use_global_device_ids=true | all-gather | bytes 409600 | tf_op jit(solution)/shard_map/all_gather | solution.py:29
  42.1 0.6 fusion.42
  43.3 26.6 %all-gather.5 = f32[8,5,4096]{2,1,0:T(8,128)S(1)} all-gather(f32[1,5,4096]{2,1,0:T(8,128)S(1)} %maximum_bitcast_fusion.2), channel_id=4, replica_groups=mesh['seq_0'=8,'seq_1'=4,'seq_2'=2,'chan'=8] {'seq_0'}, dimensions={0}, use_global_device_ids=true | all-gather | bytes 737280 | tf_op jit(solution)/shard_map/all_gather | solution.py:29
  69.9 0.8 fusion.55
  70.7 0.8 slice.187
  71.5 0.7 fusion.56
  72.2 0.7 fusion.57
  72.9 1.0 copy.188
  73.9 1.8 %fusion.18 = f32[8,4,64,256]{3,2,1,0:T(8,128)} fusion(f32[8,4,64,64]{3,2,1,0:T(8,128)S(1)} %get-tuple-element.33, bf16[8,256,64,1]{1,0,2,3:T(8,128)(2,1)S(1)} %bitcast.164), kind=kOutput, calls=%fused_computation.32 | convolution fusion | flops 67633152 | bytes 2883584 | tf_op jit(solution)/shard_map/btn,bhpn->bthp/dot_general | solution.py:86
  75.7 1.8 %fusion.29 = f32[8,4,64,256]{3,2,1,0:T(8,128)} fusion(f32[8,4,64,64]{3,2,1,0:T(8,128)S(1)} %get-tuple-element.33, bf16[8,256,64,1]{1,0,2,3:T(8,128)(2,1)S(1)} %bitcast.165), kind=kOutput, calls=%fused_computation.44 | convolution fusion | flops 67239936 | bytes 2883584 | tf_op jit(solution)/shard_map/btn,bhpn->bthp/dot_general | solution.py:83
  77.5 0.6 copy.142
  78.1 0.6 iota_compare_fusion
  79.9 0.6 fusion.53
  80.5 1.2 exp.208
  81.7 1.0 squeeze.92
  82.7 1.0 squeeze.93
  83.6 1.0 squeeze.94
  84.6 1.0 squeeze.95
  85.8 1.1 subtract_convert_fusion.2
  88.4 0.6 copy-done.1
  89.0 0.6 copy-done.2
  89.6 3.3 %fusion.14 = f32[8,256,4,64]{1,3,2,0:T(8,128)S(1)} fusion(bf16[8,256,4,64]{1,3,2,0:T(8,128)(2,1)S(1)} %copy.146, f32[8,4,64,256]{3,2,1,0:T(8,128)S(1)} %fusion.26, f32[8,4,64,256]{3,2,1,0:T(8,128)S(1)} %fusion.24, f32[8,4,64,256]{3,2,1,0:T(8,128)S(1)} %copy-done.2, f32[8,4,64,256]{3,2,1,0:T(8,128)S(1)} %copy-done.1, f32[4,8,256]{2,0,1:T(4,128)S(1)} %bitcast.181, ...), kind=kOutput, calls=%fused_computation.22 | convolution fusion | flops 285736960 | bytes 13828112 | tf_op jit(solution)/shard_map/hbts,bshp->bthp/dot_general | solution.py:131
  92.9 1.2 %copy.161 = f32[8,256,4,64]{1,0,3,2:T(8,128)S(1)} copy(f32[8,256,4,64]{1,3,2,0:T(8,128)S(1)} %fusion.14) | data formatting | bytes 4194304 | tf_op jit(solution)/shard_map/add | solution.py:137
  94.2 0.9 copy.189
  95.0 1.5 %copy.162 = bf16[2048,256]{0,1:T(8,128)(2,1)S(1)} copy(bf16[2048,256]{1,0:T(8,128)(2,1)} %param.11) | data formatting | bytes 2097152 | tf_op args[1]
  96.5 0.8 multiply_reduce_fusion
  97.4 18.1 %all_to_all.6 = f32[8,1,2048]{2,1,0:T(1,128)S(1)} all-to-all(f32[8,1,2048]{2,1,0:T(1,128)S(1)} %broadcast_in_dim.42), channel_id=1, replica_groups=mesh['seq_0'=8,'seq_1'=4,'seq_2'=2,'chan'=8] {'chan'}, dimensions={0} | all-to-all | bytes 131072 | tf_op jit(solution)/shard_map/all_to_all | solution.py:55
  115.6 1.8 %multiply_convert_fusion.2 = bf16[2048,256]{0,1:T(8,128)(2,1)} fusion(f32[256]{0:T(256)S(1)} %copy-done.26, f32[2048]{0:T(1024)S(1)} %add_rsqrt_fusion, f32[2048,256]{0,1:T(8,128)S(1)} %bitcast.162, bf16[2048,256]{0,1:T(8,128)(2,1)S(1)} %copy.162), kind=kLoop, calls=%fused_computation.25 | loop fusion | flops 4718592 | bytes 4203520 | tf_op jit(solution)/shard_map/convert_element_type | solution.py:143
  117.4 2.3 %copy.164 = bf16[2048,256]{1,0:T(8,128)(2,1)} copy(bf16[2048,256]{0,1:T(8,128)(2,1)} %multiply_convert_fusion.2) | data formatting | bytes 2097152 | tf_op jit(solution)/shard_map/convert_element_type | solution.py:143
  (134 shorter events, 6.2 us)
Async XLA Ops:
  4.0 1.8 %copy-start.6 = (f32[4,8,256]{2,1,0:T(8,128)}, f32[4,8,256]{2,1,0:T(8,128)S(1)}, u32[]{:S(2)}) copy-start(f32[4,8,256]{2,1,0:T(8,128)S(1)} %get-tuple-element.97) | copy-start | bytes 98308
  9.7 1.1 copy-start.3
  10.8 1.2 %copy-start.20 = (f32[4,8,256]{2,0,1:T(4,128)S(1)}, f32[4,8,256]{2,0,1:T(4,128)}, u32[]{:S(2)}) copy-start(f32[4,8,256]{2,0,1:T(4,128)} %copy.148) | copy-start | bytes 98308
  10.9 3.6 %copy-start = (f32[8,4,64,64]{3,2,1,0:T(8,128)S(1)}, f32[8,4,64,64]{3,2,1,0:T(8,128)}, u32[]{:S(2)}) copy-start(f32[8,4,64,64]{3,2,1,0:T(8,128)} %custom-call.1) | copy-start | bytes 1572868
  42.7 0.5 copy-start.24
  42.7 0.6 copy-start.25
  75.6 1.8 %copy-start.7 = (f32[4,8,256]{2,1,0:T(8,128)S(1)}, f32[4,8,256]{2,1,0:T(8,128)}, u32[]{:S(2)}) copy-start(f32[4,8,256]{2,1,0:T(8,128)} %copy-done.6) | copy-start | bytes 98308
  75.6 3.1 %copy-start.15 = (f32[1,4,4096]{2,1,0:T(4,128)S(1)}, f32[1,4,4096]{2,1,0:T(4,128)}, u32[]{:S(2)}) copy-start(f32[1,4,4096]{2,1,0:T(4,128)} %get-tuple-element.103) | copy-start | bytes 196612
  75.7 3.2 %copy-start.14 = (f32[1,4,4096]{2,1,0:T(4,128)S(1)}, f32[1,4,4096]{2,1,0:T(4,128)}, u32[]{:S(2)}) copy-start(f32[1,4,4096]{2,1,0:T(4,128)} %get-tuple-element.109) | copy-start | bytes 196612
  75.7 3.4 %copy-start.13 = (f32[1,4,4096]{2,1,0:T(4,128)S(1)}, f32[1,4,4096]{2,1,0:T(4,128)}, u32[]{:S(2)}) copy-start(f32[1,4,4096]{2,1,0:T(4,128)} %get-tuple-element.108) | copy-start | bytes 196612
  75.7 3.5 %copy-start.12 = (f32[1,4,4096]{2,1,0:T(4,128)S(1)}, f32[1,4,4096]{2,1,0:T(4,128)}, u32[]{:S(2)}) copy-start(f32[1,4,4096]{2,1,0:T(4,128)} %get-tuple-element.107) | copy-start | bytes 196612
  75.7 3.6 %copy-start.11 = (f32[1,4,4096]{2,1,0:T(4,128)S(1)}, f32[1,4,4096]{2,1,0:T(4,128)}, u32[]{:S(2)}) copy-start(f32[1,4,4096]{2,1,0:T(4,128)} %get-tuple-element.106) | copy-start | bytes 196612
  75.7 3.7 %copy-start.10 = (f32[1,4,4096]{2,1,0:T(4,128)S(1)}, f32[1,4,4096]{2,1,0:T(4,128)}, u32[]{:S(2)}) copy-start(f32[1,4,4096]{2,1,0:T(4,128)} %get-tuple-element.105) | copy-start | bytes 196612
  75.7 3.8 %copy-start.9 = (f32[1,4,4096]{2,1,0:T(4,128)S(1)}, f32[1,4,4096]{2,1,0:T(4,128)}, u32[]{:S(2)}) copy-start(f32[1,4,4096]{2,1,0:T(4,128)} %get-tuple-element.104) | copy-start | bytes 196612
  75.7 4.0 %copy-start.8 = (f32[1,4,4096]{2,1,0:T(4,128)S(1)}, f32[1,4,4096]{2,1,0:T(4,128)}, u32[]{:S(2)}) copy-start(f32[1,4,4096]{2,1,0:T(4,128)} %get-tuple-element.110) | copy-start | bytes 196612
  75.7 4.1 %copy-start.5 = (f32[8,1,4096]{2,1,0:T(1,128)S(1)}, f32[8,1,4096]{2,1,0:T(1,128)}, u32[]{:S(2)}) copy-start(f32[8,1,4096]{2,1,0:T(1,128)} %slice.187) | copy-start | bytes 393220
  77.5 8.1 %copy-start.17 = (f32[1,4,4096]{2,1,0:T(4,128)S(1)}, f32[1,4,4096]{2,1,0:T(4,128)}, u32[]{:S(2)}) copy-start(f32[1,4,4096]{2,1,0:T(4,128)} %get-tuple-element.115) | copy-start | bytes 196612
  77.5 8.2 %copy-start.16 = (f32[1,4,4096]{2,1,0:T(4,128)S(1)}, f32[1,4,4096]{2,1,0:T(4,128)}, u32[]{:S(2)}) copy-start(f32[1,4,4096]{2,1,0:T(4,128)} %get-tuple-element.116) | copy-start | bytes 196612
  86.9 0.9 copy-start.19
  86.9 1.0 copy-start.18
  87.0 1.0 copy-start.4
  87.4 1.6 %copy-start.1 = (f32[8,4,64,256]{3,2,1,0:T(8,128)S(1)}, f32[8,4,64,256]{3,2,1,0:T(8,128)}, u32[]{:S(2)}) copy-start(f32[8,4,64,256]{3,2,1,0:T(8,128)} %fusion.18) | copy-start | bytes 6291460
  87.4 2.2 %copy-start.2 = (f32[8,4,64,256]{3,2,1,0:T(8,128)S(1)}, f32[8,4,64,256]{3,2,1,0:T(8,128)}, u32[]{:S(2)}) copy-start(f32[8,4,64,256]{3,2,1,0:T(8,128)} %fusion.29) | copy-start | bytes 6291460
  87.4 2.2 %copy-start.21 = (pred[256,256]{1,0:T(8,128)(4,1)S(1)}, pred[256,256]{1,0:T(8,128)(4,1)}, u32[]{:S(2)}) copy-start(pred[256,256]{1,0:T(8,128)(4,1)} %iota_compare_fusion) | copy-start | bytes 196612
  87.4 2.2 %copy-start.22 = (f32[4,8,256]{2,0,1:T(4,128)S(1)}, f32[4,8,256]{2,0,1:T(4,128)}, u32[]{:S(2)}) copy-start(f32[4,8,256]{2,0,1:T(4,128)} %copy.142) | copy-start | bytes 98308
  87.4 2.2 %copy-start.23 = (f32[4,2048]{1,0:T(4,128)S(1)}, f32[4,2048]{1,0:T(4,128)}, u32[]{:S(2)}) copy-start(f32[4,2048]{1,0:T(4,128)} %param.14) | copy-start | bytes 98308
  87.4 2.2 %copy-start.27 = (f32[4]{0:T(128)S(1)}, f32[4]{0:T(128)}, u32[]{:S(2)}) copy-start(f32[4]{0:T(128)} %param.16) | copy-start | bytes 52
  96.5 19.1 %copy-start.26 = (f32[256]{0:T(256)S(1)}, f32[256]{0:T(256)}, u32[]{:S(2)}) copy-start(f32[256]{0:T(256)} %param.17) | copy-start | bytes 3076
where the time goes:
time: 120 us
  blocking collectives  62.5 us (52%)
  local copies, waits for them, and re-layouts  34.4 us (29%)
  other arithmetic  11.4 us (10%)
  matrix products  10.5 us (9%)
    all_gather x3, blocking collectives, all_in_one(): both, at, found = (lax.all_gather(jnp.concatenate(lines), axis), 0, {})  44.3 us
    all_to_all x1, blocking collectives, copy_for_each(): lax.all_to_all(jnp.broadcast_to(shard[None], (length, *shard.shape)), axi...  18.1 us
    dynamic_slice x16, local copies, waits for them, and re-layouts, per_device(): lax.scan(carry_blocks, jnp.zeros((head_count, head_width, nstate), jnp.fl...  8.12 us
    unnamed x64, local copies, waits for them, and re-layouts  5.44 us
    squeeze x14, local copies, waits for them, and re-layouts, prefix_by_axis(): total = combine(total, jax.tree.map(lambda part: part[k], pieces))  5.12 us
    reshape x2, local copies, waits for them, and re-layouts, per_device(): x_blocks = x_in.reshape(block_count, BLOCK, head_count, head_width)  4.35 us
    dot_general x1, matrix products, per_device(): jnp.einsum('hbts,bshp->bthp', weights, x_blocks, preferred_element_type=j...  3.28 us
    dot_general x1, matrix products, per_device(): jnp.einsum('bshp,hbsn->bhpn', x_blocks, decayed_b, preferred_element_type...  2.44 us

commit v1 on v0

v1 whole, which is shorter than its diff:
```python
import functools

import jax
import jax.numpy as jnp
from jax import lax
from jax.experimental import pallas as pl
from jax.experimental.pallas import tpu as pltpu
from jax.sharding import Mesh
from jax.sharding import PartitionSpec as P

CH = 2048
HEAD = 64
STATE = 64
SEQ = ("seq_0", "seq_1", "seq_2")
CUT = 128
EPSILON = 1e-05
LOG2E = 1.4426950408889634
MIB = 1024 * 1024

f32 = jnp.float32
bf16 = jnp.bfloat16
exact = functools.partial(
    jnp.dot, precision=lax.Precision.HIGHEST, preferred_element_type=f32
)


def dot(a, b):
    return jnp.dot(a, b, preferred_element_type=f32)


def dot_nt(a, b):
    return lax.dot_general(a, b, (((1,), (1,)), ((), ())), preferred_element_type=f32)


def dot_tn(a, b):
    return lax.dot_general(a, b, (((0,), (0,)), ((), ())), preferred_element_type=f32)


def iota(shape, axis):
    return lax.broadcasted_iota(jnp.int32, shape, axis)


def eye(rows, columns):
    return jnp.where(iota((rows, columns), 0) == iota((rows, columns), 1) % STATE, 1.0, 0.0)


def split3(v):
    high = v.astype(bf16).astype(f32)
    rest = v - high
    middle = rest.astype(bf16).astype(f32)
    return high, middle, rest - middle


def by_cut(ref):
    tokens = ref.shape[1]
    return jnp.concatenate([ref[:, k * CUT : (k + 1) * CUT] for k in range(tokens // CUT)], axis=0)


def two_heads(even, odd):
    return jnp.where(iota(even.shape, 1) < HEAD, even, odd)


def end_state_kernel(
    x_hbm, b_hbm, step_hbm, keep_hbm, out_ref,
    x_ref, b_ref, step_ref, keep_ref, factor, lhs, sems,
):
    copies = [
        pltpu.make_async_copy(source, target, sems.at[i])
        for i, (source, target) in enumerate(
            ((keep_hbm, keep_ref), (step_hbm, step_ref), (b_hbm, b_ref), (x_hbm, x_ref))
        )
    ]
    for copy in copies:
        copy.start()
    heads, tokens = step_ref.shape
    cuts = tokens // CUT
    row, col = iota((CUT, CUT), 0), iota((CUT, CUT), 1)
    copies[0].wait()
    keep = by_cut(keep_ref)
    after = exact(keep, jnp.where(row > col, 1.0, 0.0))
    total = exact(keep, jnp.ones((CUT, CUT), f32))
    count = heads * cuts
    row, col = iota((count, count), 0), iota((count, count), 1)
    same = row % heads == col % heads
    later = exact(jnp.where(same & (col // heads > row // heads), 1.0, 0.0), total)
    decay = jnp.exp(later[:heads] + total[:heads])
    lane = iota((1, CUT), 1) // (CUT // heads)
    decays = jnp.zeros((1, CUT), f32)
    for h in range(heads):
        decays = jnp.where(lane == h, decay[h : h + 1], decays)
    copies[1].wait()
    factor[...] = jnp.exp(after + later) * by_cut(step_ref)
    copies[2].wait()
    for k in range(cuts):
        part = b_ref[:, k * CUT : (k + 1) * CUT].astype(f32)
        for h in range(heads):
            scaled = part * factor[k * heads + h : k * heads + h + 1, :]
            lhs[h * STATE : (h + 1) * STATE, k * CUT : (k + 1) * CUT] = scaled.astype(bf16)
    copies[3].wait()
    pairs = heads // 2
    for pair in range(pairs):
        lanes = slice(pair * CUT, (pair + 1) * CUT)
        both = dot(lhs[pair * 2 * STATE : (pair + 1) * 2 * STATE, :], x_ref[:, lanes])
        out_ref[:, 0, lanes] = two_heads(both[:STATE], both[STATE:])
    out_ref[:, 0, pairs * CUT :] = jnp.broadcast_to(decays, (STATE, CUT))


def scan_kernel(heads, got_ref, _, out_ref, state_ref, decay_ref):
    count = got_ref.shape[0]
    width = heads * HEAD
    state_ref[...] = got_ref[:, 0, :width]
    row, col = iota((CUT, width), 0), iota((CUT, width), 1)
    spread = jnp.where(row == col // HEAD * (CUT // heads), 1.0, 0.0)
    decay_ref[...] = exact(got_ref[:, 0, width:], spread)
    state = jnp.zeros((1, width), f32)
    for k in range(count):
        out_ref[k] = state
        state = decay_ref[k : k + 1, :] * state + state_ref[k : k + 1, :]


def local_kernel(
    skip_ref, x_hbm, gate_hbm, b_hbm, c_hbm, step_hbm, keep_hbm,
    base_ref, carry_ref, flag_ref,
    x_ref, gate_ref, b_ref, c_ref, step_ref, keep_ref,
    left, offset, factor, decays, starts, state, sems, x_sems, gate_sems,
):
    copies = [
        pltpu.make_async_copy(source, target, sems.at[i])
        for i, (source, target) in enumerate(
            ((keep_hbm, keep_ref), (step_hbm, step_ref), (b_hbm, b_ref), (c_hbm, c_ref))
        )
    ]
    for copy in copies:
        copy.start()

    def tiles(k):
        at = pl.ds(pl.multiple_of(k * CUT, CUT), CUT)
        return (
            pltpu.make_async_copy(x_hbm.at[at], x_ref.at[at], x_sems.at[k]),
            pltpu.make_async_copy(gate_hbm.at[at], gate_ref.at[at], gate_sems.at[k]),
        )

    def start(k, _):
        for copy in tiles(k):
            copy.start()
        return 0

    lax.fori_loop(0, x_hbm.shape[0] // CUT, start, 0)
    flag_ref[...] = jnp.zeros_like(flag_ref)
    for copy in copies:
        copy.wait()
    heads, tokens = step_ref.shape
    channels = x_ref.shape[1]
    cuts = tokens // CUT
    count = heads * cuts
    keep = by_cut(keep_ref)
    step = by_cut(step_ref)
    row, col = iota((CUT, CUT), 0), iota((CUT, CUT), 1)
    upto = exact(keep, jnp.where(row <= col, 1.0, 0.0)) * LOG2E
    after = exact(keep, jnp.where(row > col, 1.0, 0.0))
    total = exact(keep, jnp.ones((CUT, CUT), f32))
    big_row, big_col = iota((count, count), 0), iota((count, count), 1)
    same = big_row % heads == big_col % heads
    before = exact(jnp.where(same & (big_col // heads < big_row // heads), 1.0, 0.0), total)
    factor[...] = jnp.exp(after) * step
    decays[...] = jnp.exp(total)
    starts[...] = jnp.exp(before)
    pieces = split3(upto)
    minus = split3(jnp.log2(jnp.maximum(step, 1e-37)) - upto)
    for k in range(cuts):
        at = slice(k * heads, (k + 1) * heads)
        left[k] = jnp.concatenate([piece[at] for piece in pieces] + [jnp.ones((4, CUT), f32)], axis=0)
        rows = [
            jnp.concatenate([piece[k * heads + h : k * heads + h + 1] for h in range(heads)], axis=1)
            for piece in minus
        ]
        offset[k] = jnp.concatenate(rows + [jnp.zeros((1, heads * CUT), f32)], axis=0)
    state[...] = jnp.zeros_like(state)
    double = eye(STATE, 2 * STATE).astype(bf16)
    pick_row, pick_col = iota((12, heads * CUT), 0), iota((12, heads * CUT), 1)
    pick = jnp.where(pick_row % heads == pick_col // CUT, 1.0, 0.0)
    wide_row, wide_col = iota((16, channels), 0), iota((16, channels), 1)
    wide = jnp.where((wide_row % heads == wide_col // HEAD) & (wide_row < 12), 1.0, 0.0)
    lane_head = iota((1, channels), 1) // HEAD
    only = [jnp.where(lane_head == h, 1.0, 0.0).astype(bf16) for h in range(heads)]
    skip = jnp.zeros((1, channels), f32)
    for h in range(heads):
        skip = jnp.where(lane_head == h, skip_ref[h], skip)

    def per_channel(ref, first):
        wide_rows = [
            two_heads(ref[pl.ds(first + 2 * p, 1), :], ref[pl.ds(first + 2 * p + 1, 1), :])
            for p in range(heads // 2)
        ]
        return jnp.concatenate(wide_rows, axis=1)

    def one_cut(k, _):
        at = pl.ds(pl.multiple_of(k * CUT, CUT), CUT)
        first = k * heads
        for copy in tiles(k):
            copy.wait()
        x = x_ref[at, :]
        b = b_ref[:, at]
        twice = dot_tn(c_ref[:, at], double).astype(bf16)
        lhs = jnp.transpose(left[k]).astype(bf16)
        rhs = jnp.concatenate([jnp.concatenate([pick, offset[k]], axis=0), wide], axis=1).astype(bf16)
        gaps = dot(lhs, rhs)
        scores = jnp.where(row >= col, dot(twice[:, :STATE], b), 0.0)
        weights = [
            (scores * jnp.exp2(jnp.minimum(gaps[:, h * CUT : (h + 1) * CUT], 0.0))).astype(bf16)
            for h in range(heads)
        ]
        inside = dot(
            jnp.concatenate(weights, axis=1), jnp.concatenate([x * mask for mask in only], axis=0)
        )
        now = state[...]
        high = now.astype(bf16)
        low = (now - high.astype(f32)).astype(bf16)
        earlier = dot(twice, jnp.concatenate([high, low], axis=0))
        growth = jnp.exp2(gaps[:, heads * CUT :])
        gate = gate_ref[at, :].astype(f32)
        gate = gate / (1.0 + jnp.exp(-gate))
        base_ref[at, :] = (inside + growth * earlier + skip * x.astype(f32)) * gate
        carry_ref[at, :] = (growth * per_channel(starts, first) * gate).astype(bf16)
        b_turned = b.astype(f32)
        ends = []
        for pair in range(heads // 2):
            scaled = [
                b_turned * factor[pl.ds(first + 2 * pair + i, 1), :] for i in range(2)
            ]
            both = dot(
                jnp.concatenate(scaled, axis=0).astype(bf16), x[:, pair * CUT : (pair + 1) * CUT]
            )
            ends.append(two_heads(both[:STATE], both[STATE:]))
        state[...] = per_channel(decays, first) * now + jnp.concatenate(ends, axis=1)
        return 0

    lax.fori_loop(0, cuts, one_cut, 0)


def gate_kernel(got_ref, c_ref, base_ref, carry_ref, gated_ref, squares_ref):
    peers = squares_ref.shape[0]
    tokens = base_ref.shape[0]
    now = got_ref[:, 0, :]
    high = now.astype(bf16)
    low = (now - high.astype(f32)).astype(bf16)
    both = jnp.concatenate([high, low], axis=0)
    ones = jnp.ones((8, 2 * CUT), bf16)
    size = 2 * CUT
    for k in range(tokens // size):
        at = slice(k * size, (k + 1) * size)
        c = c_ref[:, at]
        added = dot_tn(jnp.concatenate([c, c], axis=0), both)
        gated = base_ref[at, :] + carry_ref[at, :].astype(f32) * added
        gated_ref[at, :] = gated
        square = gated * gated
        square = square[:, :CUT] + square[:, CUT:]
        high = square.astype(bf16)
        low = (square - high.astype(f32)).astype(bf16)
        summed = dot_nt(ones, jnp.concatenate([high, low], axis=1))
        for peer in range(peers):
            for half in range(2):
                squares_ref[peer, 2 * k + half : 2 * k + half + 1, :] = summed[
                    :1, half * CUT : (half + 1) * CUT
                ]


def norm_kernel(got_ref, gain_ref, gated_ref, out_hbm, out_ref, sems):
    peers = got_ref.shape[0]
    cuts = got_ref.shape[1]
    summed = got_ref[0]
    for peer in range(1, peers):
        summed = summed + got_ref[peer]
    pieces = split3(lax.rsqrt(summed / CH + EPSILON))
    gain = gain_ref[...]
    ones = jnp.where(iota((8, gain.shape[1]), 0) < 3, 1.0, 0.0).astype(bf16)
    copies = []
    for k in range(cuts):
        at = slice(k * CUT, (k + 1) * CUT)
        rows = [piece[k : k + 1] for piece in pieces] + [jnp.zeros((5, CUT), f32)]
        factor = dot(jnp.transpose(jnp.concatenate(rows, axis=0)).astype(bf16), ones)
        out_ref[at, :] = (gated_ref[at, :] * factor * gain).astype(bf16)
        if k % 4 == 3:
            four = pl.ds((k - 3) * CUT, 4 * CUT)
            copy = pltpu.make_async_copy(out_ref.at[four], out_hbm.at[four], sems.at[k // 4])
            copy.start()
            copies.append(copy)
    for copy in copies:
        copy.wait()


VMEM = pl.BlockSpec(memory_space=pltpu.VMEM)
SMEM = pl.BlockSpec(memory_space=pltpu.SMEM)
HBM = pl.BlockSpec(memory_space=pltpu.HBM)


def call(kernel, out_shape, in_specs, scratch=(), out_specs=None, flops=1000000):
    return pl.pallas_call(
        kernel,
        out_shape=out_shape,
        in_specs=in_specs,
        out_specs=out_specs or jax.tree.map(lambda _: VMEM, out_shape),
        scratch_shapes=list(scratch),
        cost_estimate=pl.CostEstimate(flops=flops, bytes_accessed=4 * MIB, transcendentals=0),
        compiler_params=pltpu.CompilerParams(vmem_limit_bytes=16 * MIB),
    )


def per_device(x_in, gate_in, b_in, c_in, step_size, log_keep, skip_gain, norm_gain):
    tokens, channels = x_in.shape
    heads = step_size.shape[0]
    cuts = tokens // CUT
    shape = jax.ShapeDtypeStruct
    dma = pltpu.SemaphoreType.DMA
    b_turned, c_turned = b_in.T, c_in.T
    x_in, gate_in, b_turned, c_far, step_size, log_keep, skip_gain = (
        pltpu.with_memory_space_constraint(v, pltpu.HBM)
        for v in (x_in, gate_in, b_turned, c_turned, step_size, log_keep, skip_gain)
    )
    rows = pltpu.VMEM((heads * cuts, CUT), f32)
    wide = pltpu.VMEM((tokens, channels), bf16)
    turned = pltpu.VMEM((STATE, tokens), bf16)
    small = pltpu.VMEM((heads, tokens), f32)
    message = call(
        end_state_kernel,
        shape((STATE, 1, channels + CUT), f32),
        [HBM] * 4,
        [wide, turned, small, small, rows, pltpu.VMEM((heads * STATE, tokens), bf16), dma((4,))],
        flops=2 * tokens * STATE * channels,
    )(x_in, b_turned, step_size, log_keep)
    got = lax.all_to_all(message, SEQ, 0, 0, tiled=True)
    base, carry, flag = call(
        local_kernel,
        (shape((tokens, channels), f32), shape((tokens, channels), bf16), shape((8, CUT), f32)),
        [SMEM] + [HBM] * 6,
        [wide, wide, turned, turned, small, small]
        + [pltpu.VMEM((cuts, 16, CUT), f32), pltpu.VMEM((cuts, 4, heads * CUT), f32)]
        + [rows] * 3
        + [pltpu.VMEM((STATE, channels), f32), dma((4,)), dma((cuts,)), dma((cuts,))],
        flops=int(5e9),
    )(skip_gain, x_in, gate_in, b_turned, c_far, step_size, log_keep)
    row = pltpu.VMEM((STATE, channels), f32)
    before = call(
        functools.partial(scan_kernel, heads),
        shape((STATE, 1, channels), f32),
        [VMEM] * 2,
        [row, row],
    )(got, flag)
    entering = lax.all_to_all(before, SEQ, 0, 0, tiled=True)
    peers = lax.axis_size("chan")
    gated, squares = call(
        gate_kernel,
        (shape((tokens, channels), f32), shape((peers, cuts, CUT), f32)),
        [VMEM] * 4,
        flops=2 * tokens * STATE * channels,
    )(entering, c_turned, base, carry)
    summed = lax.all_to_all(squares, "chan", 0, 0, tiled=True)
    return call(
        norm_kernel,
        shape((tokens, channels), bf16),
        [VMEM] * 3,
        [wide, dma((4,))],
        out_specs=HBM,
    )(summed, norm_gain.reshape(1, channels), gated)


def solution(mesh):
    chan = mesh.shape["chan"]
    split = Mesh(mesh.devices.reshape(8, 4, 2, chan), (*SEQ, "chan"))
    placed = (
        P(SEQ, "chan"),
        P(SEQ, "chan"),
        P(SEQ, None),
        P(SEQ, None),
        P("chan", SEQ),
        P("chan", SEQ),
        P("chan"),
        P("chan"),
    )
    return jax.shard_map(
        per_device, mesh=split, in_specs=placed, out_specs=P(SEQ, "chan"), check_vma=False
    )
```

time: 120 us -> 65.2 us (0.54)
  the two profiles are of different devices: /device:TPU:2 before, /device:TPU:1 now
where the time goes in v1:
time: 65.2 us; the launch traced here: 65 us
  blocking collectives  37.2 us (57%)
  Pallas kernels  16 us (25%)
  starting transfers between devices  11.6 us (18%)
    all_to_all x1, blocking collectives, per_device(): entering = lax.all_to_all(before, SEQ, 0, 0, tiled=True)  20.2 us
    all_to_all x1, blocking collectives, per_device(): summed = lax.all_to_all(squares, 'chan', 0, 0, tiled=True)  17.1 us
    all_to_all x1, starting transfers between devices, per_device(): got = lax.all_to_all(message, SEQ, 0, 0, tiled=True)  11.6 us
    pallas_call x1, Pallas kernels, per_device(): call(local_kernel, (shape((tokens, channels), f32), shape((tokens, channe...  10.7 us
    pallas_call x1, Pallas kernels, per_device(): call(end_state_kernel, shape((STATE, 1, channels + CUT), f32), [HBM] * 4,...  2.76 us
    pallas_call x1, Pallas kernels, per_device(): call(norm_kernel, shape((tokens, channels), bf16), [VMEM] * 3, [wide, dma...  1.31 us
  transfers between devices with their start and end apart: 1, of which 0 were waited for; matrix products, arithmetic and copies ran while one was open for 0% of the time, Pallas kernels for 16%

profile of v1, /device:TPU:1, one launch (start us, length us, event | category | flops | bytes accessed | tf_op | source)
XLA Modules:
  0.0 65.0 jit_solution(11001087817084771252)
XLA Ops:
  0.0 2.8 %shard_map.82 = f32[64,1,384]{2,1,0:T(1,128)} custom-call(bf16[2048,256]{1,0:T(8,128)(2,1)} %x_hbm.3, bf16[64,2048]{1,0:T(8,128)(2,1)} %bitcast.6, f32[4,2048]{1,0:T(4,128)} %step_hbm.3, f32[4,2048]{1,0:T(4,128)} %keep_hbm.3), custom_call_target="tpu_custom_call" | custom-call | flops 67108864 | bytes 4194304 | tf_op jit(solution)/shard_map/pallas_call | solution.py:324
  2.8 11.6 %all-to-all-start = ((f32[64,1,384]{2,1,0:T(1,128)}), f32[64,1,384]{2,1,0:T(1,128)S(1)}, u32[]{:S(2)}, u32[]{:S(2)}) async-start(f32[64,1,384]{2,1,0:T(1,128)} %shard_map.82), calls=%async_computation | async-start | bytes 196608 | tf_op jit(solution)/shard_map/all_to_all | solution.py:331
  14.4 0.0 copy-start
  14.4 10.7 %shard_map.83 = (f32[2048,256]{1,0:T(8,128)S(1)}, bf16[2048,256]{1,0:T(8,128)(2,1)S(1)}, f32[8,128]{1,0:T(8,128)S(1)}) custom-call(f32[4]{0:T(128)} %skip_ref.1, bf16[2048,256]{1,0:T(8,128)(2,1)} %x_hbm.3, bf16[2048,256]{1,0:T(8,128)(2,1)} %gate_hbm.1, bf16[64,2048]{1,0:T(8,128)(2,1)} %bitcast.7, bf16[64,2048]{1,0:T(8,128)(2,1)} %bitcast.3, ...), custom_call_target="tpu_custom_call" | custom-call | flops 5000000000 | bytes 4194304 | tf_op jit(solution)/shard_map/pallas_call | solution.py:332
  25.1 0.0 copy-start.1
  25.1 0.0 all-to-all-done.got_ref
  25.1 0.3 shard_map.84
  25.4 20.2 %all_to_all.15.got_ref = f32[64,1,256]{2,1,0:T(1,128)S(1)} all-to-all(f32[64,1,256]{2,1,0:T(1,128)S(1)} %shard_map.84), channel_id=1, replica_groups=mesh['seq_0'=8,'seq_1'=4,'seq_2'=2,'chan'=8] {'seq_0','seq_1','seq_2'}, dimensions={0} | all-to-all | bytes 131072 | tf_op jit(solution)/shard_map/all_to_all | solution.py:349
  45.6 0.0 copy-done
  45.6 1.0 %shard_map.85 = (f32[2048,256]{1,0:T(8,128)S(1)}, f32[8,16,128]{2,1,0:T(8,128)S(1)}) custom-call(f32[64,1,256]{2,1,0:T(1,128)S(1)} %all_to_all.15.got_ref, bf16[64,2048]{1,0:T(8,128)(2,1)S(1)} %bitcast.4, f32[2048,256]{1,0:T(8,128)S(1)} %get-tuple-element.11.base_ref, bf16[2048,256]{1,0:T(8,128)(2,1)S(1)} %get-tuple-element.12.carry_ref), custom_call_target="tpu_custom_call" | custom-call | flops 67108864 | bytes 4194304 | tf_op jit(solution)/shard_map/pallas_call | solution.py:351
  46.6 17.1 %all_to_all.16.got_ref = f32[8,16,128]{2,1,0:T(8,128)S(1)} all-to-all(f32[8,16,128]{2,1,0:T(8,128)S(1)} %get-tuple-element.13), channel_id=1, replica_groups=mesh['seq_0'=8,'seq_1'=4,'seq_2'=2,'chan'=8] {'chan'}, dimensions={0} | all-to-all | bytes 131072 | tf_op jit(solution)/shard_map/all_to_all | solution.py:357
  63.7 0.0 copy-done.1
  63.7 1.3 %shard_map.86 = bf16[2048,256]{1,0:T(8,128)(2,1)} custom-call(f32[8,16,128]{2,1,0:T(8,128)S(1)} %all_to_all.16.got_ref, f32[1,256]{1,0:T(1,128)S(1)} %bitcast.5, f32[2048,256]{1,0:T(8,128)S(1)} %get-tuple-element.14.gated_ref), custom_call_target="tpu_custom_call" | custom-call | flops 1000000 | bytes 4194304 | tf_op jit(solution)/shard_map/pallas_call | solution.py:358
Async XLA Ops:
  2.8 22.3 %all-to-all-start = ((f32[64,1,384]{2,1,0:T(1,128)}), f32[64,1,384]{2,1,0:T(1,128)S(1)}, u32[]{:S(2)}, u32[]{:S(2)}) async-start(f32[64,1,384]{2,1,0:T(1,128)} %shard_map.82), calls=%async_computation | async-start | bytes 196608 | tf_op jit(solution)/shard_map/all_to_all | solution.py:331
  14.4 31.2 %copy-start = (bf16[2048,64]{0,1:T(8,128)(2,1)S(1)}, bf16[2048,64]{0,1:T(8,128)(2,1)}, u32[]{:S(2)}) copy-start(bf16[2048,64]{0,1:T(8,128)(2,1)} %param.11) | copy-start | bytes 786436
  25.1 38.6 %copy-start.1 = (f32[256]{0:T(256)S(1)}, f32[256]{0:T(256)}, u32[]{:S(2)}) copy-start(f32[256]{0:T(256)} %param.15) | copy-start | bytes 3076

commit v2 on v1

v2 whole, which is shorter than its diff:
```python
import functools

import jax
import jax.numpy as jnp
from jax import lax
from jax.experimental import pallas as pl
from jax.experimental.pallas import tpu as pltpu
from jax.sharding import Mesh
from jax.sharding import PartitionSpec as P

CH = 2048
HEAD = 64
STATE = 64
SEQ = ("seq_0", "seq_1", "seq_2")
CUT = 128
EPSILON = 1e-05
LOG2E = 1.4426950408889634
MIB = 1024 * 1024
UNROLL = 4

f32 = jnp.float32
bf16 = jnp.bfloat16
exact = functools.partial(
    jnp.dot, precision=lax.Precision.HIGHEST, preferred_element_type=f32
)


def dot(a, b):
    return jnp.dot(a, b, preferred_element_type=f32)


def dot_nt(a, b):
    return lax.dot_general(a, b, (((1,), (1,)), ((), ())), preferred_element_type=f32)


def dot_tn(a, b):
    return lax.dot_general(a, b, (((0,), (0,)), ((), ())), preferred_element_type=f32)


def iota(shape, axis):
    return lax.broadcasted_iota(jnp.int32, shape, axis)


def split3(v):
    high = v.astype(bf16).astype(f32)
    rest = v - high
    middle = rest.astype(bf16).astype(f32)
    return high, middle, rest - middle


def sum_of_pieces(v, zeros_and_ones):
    ones = zeros_and_ones.astype(bf16)
    high, middle, low = (dot(piece.astype(bf16), ones) for piece in split3(v))
    return high + (middle + low)


def by_cut(ref):
    tokens = ref.shape[1]
    return jnp.concatenate([ref[:, k * CUT : (k + 1) * CUT] for k in range(tokens // CUT)], axis=0)


def two_heads(even, odd):
    return jnp.where(iota(even.shape, 1) < HEAD, even, odd)


def end_state_kernel(
    x_hbm, b_hbm, c_hbm, step_hbm, keep_hbm,
    out_ref, x_ref, b_ref, c_ref, step_ref, keep_ref,
    x_rest, factor, lhs, sems,
):
    half = x_ref.shape[0]
    copies = [
        pltpu.make_async_copy(source, target, sems.at[i])
        for i, (source, target) in enumerate(
            (
                (keep_hbm, keep_ref),
                (step_hbm, step_ref),
                (b_hbm, b_ref),
                (x_hbm.at[pl.ds(0, half)], x_ref),
                (x_hbm.at[pl.ds(half, half)], x_rest),
                (c_hbm, c_ref),
            )
        )
    ]
    for copy in copies:
        copy.start()
    heads, tokens = step_ref.shape
    cuts = tokens // CUT
    row, col = iota((CUT, 2 * CUT), 0), iota((CUT, 2 * CUT), 1)
    kept = jnp.where((row > col) | (col >= CUT), 1.0, 0.0)
    copies[0].wait()
    sums = sum_of_pieces(by_cut(keep_ref), kept)
    after, total = sums[:, :CUT], sums[:, CUT:]
    count = heads * cuts
    row, col = iota((count, count), 0), iota((count, count), 1)
    same = row % heads == col % heads
    later = exact(jnp.where(same & (col // heads > row // heads), 1.0, 0.0), total)
    decay = jnp.exp(later[:heads] + total[:heads])
    lane = iota((1, CUT), 1) // (CUT // heads)
    decays = jnp.zeros((1, CUT), f32)
    for h in range(heads):
        decays = jnp.where(lane == h, decay[h : h + 1], decays)
    copies[1].wait()
    factor[...] = jnp.exp(after + later) * by_cut(step_ref)
    copies[2].wait()
    for k in range(cuts):
        part = b_ref[:, k * CUT : (k + 1) * CUT].astype(f32)
        for h in range(heads):
            scaled = part * factor[k * heads + h : k * heads + h + 1, :]
            lhs[h * STATE : (h + 1) * STATE, k * CUT : (k + 1) * CUT] = scaled.astype(bf16)
    copies[3].wait()
    copies[4].wait()
    pairs = heads // 2
    for pair in range(pairs):
        lanes = slice(pair * CUT, (pair + 1) * CUT)
        rows = slice(pair * 2 * STATE, (pair + 1) * 2 * STATE)
        both = dot(lhs[rows, :half], x_ref[:, lanes]) + dot(lhs[rows, half:], x_rest[:, lanes])
        out_ref[:, 0, lanes] = two_heads(both[:STATE], both[STATE:])
    out_ref[:, 0, pairs * CUT :] = jnp.broadcast_to(decays, (STATE, CUT))
    copies[5].wait()


def scan_kernel(heads, got_ref, _, out_ref, flag_ref, state_ref, decay_ref):
    flag_ref[...] = jnp.zeros_like(flag_ref)
    count = got_ref.shape[0]
    width = heads * HEAD
    state_ref[...] = got_ref[:, 0, :width]
    row, col = iota((CUT, width), 0), iota((CUT, width), 1)
    spread = jnp.where(row == col // HEAD * (CUT // heads), 1.0, 0.0)
    decay_ref[...] = exact(got_ref[:, 0, width:], spread)
    state = jnp.zeros((1, width), f32)
    for k in range(count):
        out_ref[k] = state
        state = decay_ref[k : k + 1, :] * state + state_ref[k : k + 1, :]


def tile_copies(skipped, pairs, sems):
    def copies(k):
        source = pl.ds(pl.multiple_of((skipped + k) * CUT, CUT), CUT)
        at = pl.ds(pl.multiple_of(k * CUT, CUT), CUT)
        return [
            pltpu.make_async_copy(far.at[source], near.at[at], sems.at[i, k])
            for i, (far, near) in enumerate(pairs)
        ]

    def wait(k):
        for copy in copies(k):
            copy.wait()

    for k in range(pairs[0][1].shape[0] // CUT):
        for copy in copies(k):
            copy.start()
    return wait


def early_kernel(
    skip_ref, x_ref, b_ref, c_ref, step_ref, keep_ref, gate_hbm,
    base_ref, carry_ref, state_out, gate_ref, *rest,
):
    *scratch, state, sems = rest
    wait = tile_copies(0, [(gate_hbm, gate_ref)], sems)
    state[...] = jnp.zeros_like(state)
    cut_by_cut(
        0, skip_ref, x_ref, gate_ref, b_ref, c_ref, step_ref, keep_ref, base_ref, carry_ref,
        *scratch, state, wait, lambda: None,
    )
    state_out[...] = state[...]


def late_kernel(
    flag_ref, state_in, skip_ref, x_hbm, b_hbm, c_hbm, step_hbm, keep_hbm, gate_hbm,
    base_ref, carry_ref, gate_ref, *rest,
):
    *scratch, state, sems, x_ref, b_ref, c_ref, step_ref, keep_ref, more_sems = rest
    copies = [
        pltpu.make_async_copy(far, near, more_sems.at[i])
        for i, (far, near) in enumerate(
            ((keep_hbm, keep_ref), (step_hbm, step_ref), (b_hbm, b_ref), (c_hbm, c_ref))
        )
    ]
    for copy in copies:
        copy.start()
    skipped = x_ref.shape[0] // CUT
    wait = tile_copies(skipped, [(x_hbm, x_ref), (gate_hbm, gate_ref)], sems)
    state[...] = state_in[...]
    copies[0].wait()
    copies[1].wait()

    def wait_both():
        copies[2].wait()
        copies[3].wait()

    cut_by_cut(
        skipped, skip_ref, x_ref, gate_ref, b_ref, c_ref, step_ref, keep_ref,
        base_ref, carry_ref, *scratch, state, wait, wait_both,
    )


def cut_by_cut(
    skipped, skip_ref, x_ref, gate_ref, b_ref, c_ref, step_ref, keep_ref, base_ref, carry_ref,
    left, offset, factor, decays, starts, state, wait_tile, wait_rest,
):
    heads, tokens = step_ref.shape
    cuts = tokens // CUT
    mine = x_ref.shape[0] // CUT
    count = heads * cuts
    step = by_cut(step_ref)
    row, col = iota((CUT, 3 * CUT), 0), iota((CUT, 3 * CUT), 1)
    kind = col // CUT
    kept = (kind == 2) | ((kind == 0) & (row <= col)) | ((kind == 1) & (row > col - CUT))
    sums = sum_of_pieces(by_cut(keep_ref), jnp.where(kept, 1.0, 0.0))
    upto, after, total = (sums[:, i * CUT : (i + 1) * CUT] for i in range(3))
    upto = upto * LOG2E
    row, col = iota((count, count), 0), iota((count, count), 1)
    earlier_cut = (row % heads == col % heads) & (col // heads < row // heads)
    factor[...] = jnp.exp(after) * step
    decays[...] = jnp.exp(total)
    starts[...] = jnp.exp(exact(jnp.where(earlier_cut, 1.0, 0.0), total))
    offset[...] = jnp.log2(jnp.maximum(step, 1e-37)) - upto
    for k in range(mine):
        rows = upto[(skipped + k) * heads : (skipped + k + 1) * heads]
        left[k] = jnp.concatenate([rows, jnp.zeros((8 - heads, CUT), f32)], axis=0)
    row, col = iota((CUT, CUT), 0), iota((CUT, CUT), 1)
    causal = row >= col
    low_lanes = jnp.where(iota((1, CUT), 1) < HEAD, 1.0, 0.0)
    only = [low_lanes.astype(bf16), (1.0 - low_lanes).astype(bf16)]

    def one_cut(k, _):
        at = pl.ds(pl.multiple_of(k * CUT, CUT), CUT)
        far = pl.ds(pl.multiple_of((skipped + k) * CUT, CUT), CUT)
        first = (skipped + k) * heads
        wait_tile(k)
        b = b_ref[:, far]
        c = jnp.transpose(c_ref[:, far])
        growths = jnp.transpose(left[k])
        growths = [jnp.broadcast_to(growths[:, h : h + 1], (CUT, CUT)) for h in range(heads)]
        scores = jnp.where(causal, dot(c, b), 0.0)
        b_turned = b.astype(f32)
        now = state[...]
        high = now.astype(bf16)
        low = (now - high.astype(f32)).astype(bf16)
        earlier = dot(jnp.concatenate([c, c], axis=1), jnp.concatenate([high, low], axis=0))
        for pair in range(heads // 2):
            lanes = slice(pair * CUT, (pair + 1) * CUT)
            x = x_ref[at, lanes]
            weights = []
            for h in range(2 * pair, 2 * pair + 2):
                gaps = growths[h] + offset[pl.ds(first + h, 1), :]
                weights.append((scores * jnp.exp2(jnp.minimum(gaps, 0.0))).astype(bf16))
            inside = dot(
                jnp.concatenate(weights, axis=1), jnp.concatenate([x * mask for mask in only], axis=0)
            )
            growth = jnp.exp2(two_heads(growths[2 * pair], growths[2 * pair + 1]))
            gate = gate_ref[at, lanes].astype(f32)
            gate = gate * pl.reciprocal(1.0 + jnp.exp(-gate))
            skip = two_heads(
                jnp.full((1, CUT), skip_ref[2 * pair]), jnp.full((1, CUT), skip_ref[2 * pair + 1])
            )
            base_ref[at, lanes] = (inside + growth * earlier[:, lanes] + skip * x.astype(f32)) * gate

            def per_channel(ref):
                even = first + 2 * pair
                return two_heads(ref[pl.ds(even, 1), :], ref[pl.ds(even + 1, 1), :])

            carry_ref[at, lanes] = (growth * per_channel(starts) * gate).astype(bf16)
            scaled = [b_turned * factor[pl.ds(first + 2 * pair + i, 1), :] for i in range(2)]
            both = dot(jnp.concatenate(scaled, axis=0).astype(bf16), x)
            state[:, lanes] = per_channel(decays) * now[:, lanes] + two_heads(both[:STATE], both[STATE:])
        return 0

    wait_rest()
    lax.fori_loop(0, mine, one_cut, 0, unroll=UNROLL)


def gate_kernel(got_ref, c_ref, *refs):
    *parts, gated_ref, squares_ref = refs
    peers = squares_ref.shape[0]
    tokens = gated_ref.shape[0]
    now = got_ref[:, 0, :]
    high = now.astype(bf16)
    low = (now - high.astype(f32)).astype(bf16)
    both = jnp.concatenate([high, low], axis=0)
    ones = jnp.ones((8, 2 * CUT), bf16)
    size = 2 * CUT
    half_tokens = tokens // (len(parts) // 2)
    for k in range(tokens // size):
        at = slice(k * size, (k + 1) * size)
        c = c_ref[:, at]
        added = dot_tn(jnp.concatenate([c, c], axis=0), both)
        first = k * size
        base_ref, carry_ref = parts[2 * (first // half_tokens) : 2 * (first // half_tokens) + 2]
        here = slice(first % half_tokens, first % half_tokens + size)
        gated = base_ref[here, :] + carry_ref[here, :].astype(f32) * added
        gated_ref[at, :] = gated
        square = gated * gated
        square = square[:, :CUT] + square[:, CUT:]
        high = square.astype(bf16)
        low = (square - high.astype(f32)).astype(bf16)
        summed = dot_nt(ones, jnp.concatenate([high, low], axis=1))
        for peer in range(peers):
            for half in range(2):
                squares_ref[peer, 2 * k + half : 2 * k + half + 1, :] = summed[
                    :1, half * CUT : (half + 1) * CUT
                ]


def norm_kernel(got_ref, gain_ref, gated_ref, out_hbm, out_ref, sems):
    peers = got_ref.shape[0]
    cuts = got_ref.shape[1]
    summed = got_ref[0]
    for peer in range(1, peers):
        summed = summed + got_ref[peer]
    pieces = split3(lax.rsqrt(summed / CH + EPSILON))
    gain = gain_ref[...]
    ones = jnp.where(iota((8, gain.shape[1]), 0) < 3, 1.0, 0.0).astype(bf16)
    copies = []
    for k in range(cuts):
        at = slice(k * CUT, (k + 1) * CUT)
        rows = [piece[k : k + 1] for piece in pieces] + [jnp.zeros((5, CUT), f32)]
        factor = dot(jnp.transpose(jnp.concatenate(rows, axis=0)).astype(bf16), ones)
        out_ref[at, :] = (gated_ref[at, :] * factor * gain).astype(bf16)
        if k % 4 == 3:
            four = pl.ds((k - 3) * CUT, 4 * CUT)
            copy = pltpu.make_async_copy(out_ref.at[four], out_hbm.at[four], sems.at[k // 4])
            copy.start()
            copies.append(copy)
    for copy in copies:
        copy.wait()


VMEM = pl.BlockSpec(memory_space=pltpu.VMEM)
SMEM = pl.BlockSpec(memory_space=pltpu.SMEM)
HBM = pl.BlockSpec(memory_space=pltpu.HBM)


def call(kernel, out_shape, in_specs, scratch=(), out_specs=None, flops=1000000):
    return pl.pallas_call(
        kernel,
        out_shape=out_shape,
        in_specs=in_specs,
        out_specs=out_specs or jax.tree.map(lambda _: VMEM, out_shape),
        scratch_shapes=list(scratch),
        cost_estimate=pl.CostEstimate(flops=flops, bytes_accessed=4 * MIB, transcendentals=0),
        compiler_params=pltpu.CompilerParams(vmem_limit_bytes=16 * MIB),
    )


def per_device(x_in, gate_in, b_in, c_in, step_size, log_keep, skip_gain, norm_gain):
    tokens, channels = x_in.shape
    heads = step_size.shape[0]
    cuts = tokens // CUT
    shape = jax.ShapeDtypeStruct
    dma = pltpu.SemaphoreType.DMA
    b_turned, c_turned = b_in.T, c_in.T
    x_in, gate_in, b_turned, c_far, step_size, log_keep, skip_gain = (
        pltpu.with_memory_space_constraint(v, pltpu.HBM)
        for v in (x_in, gate_in, b_turned, c_turned, step_size, log_keep, skip_gain)
    )
    rows = pltpu.VMEM((heads * cuts, CUT), f32)
    half = tokens // 2
    row = pltpu.VMEM((STATE, channels), f32)
    part = shape((half, channels), bf16)
    turned = shape((STATE, tokens), bf16)
    per_head = shape((heads, tokens), f32)
    near_shapes = (turned, turned, per_head, per_head)
    local_shapes = (shape((half, channels), f32), part)
    half_wide = pltpu.VMEM((half, channels), bf16)
    local_scratch = [
        half_wide,
        pltpu.VMEM((cuts // 2, 8, CUT), f32),
        rows,
        rows, rows, rows, row,
    ]
    message, x_near, *near = call(
        end_state_kernel,
        (shape((STATE, 1, channels + CUT), f32), part, *near_shapes),
        [HBM] * 5,
        [half_wide, rows, pltpu.VMEM((heads * STATE, tokens), bf16), dma((6,))],
        flops=2 * tokens * STATE * channels,
    )(x_in, b_turned, c_far, step_size, log_keep)
    got = lax.all_to_all(message, SEQ, 0, 0, tiled=True)
    base_0, carry_0, state = call(
        early_kernel,
        (*local_shapes, shape((STATE, channels), f32)),
        [SMEM] + [VMEM] * 5 + [HBM],
        [*local_scratch, dma((1, cuts // 2))],
        flops=int(5e9),
    )(skip_gain, x_near, *near, gate_in)
    before, flag = call(
        functools.partial(scan_kernel, heads),
        (shape((STATE, 1, channels), f32), shape((8, CUT), f32)),
        [VMEM] * 2,
        [row, row],
    )(got, state)
    entering = lax.all_to_all(before, SEQ, 0, 0, tiled=True)
    base_1, carry_1 = call(
        late_kernel,
        local_shapes,
        [VMEM] * 2 + [SMEM] + [HBM] * 6,
        [
            *local_scratch, dma((2, cuts // 2)), half_wide,
            *(pltpu.VMEM(v.shape, v.dtype) for v in near_shapes), dma((4,)),
        ],
        flops=int(5e9),
    )(flag, state, skip_gain, x_in, b_turned, c_far, step_size, log_keep, gate_in)
    peers = lax.axis_size("chan")
    gated, squares = call(
        gate_kernel,
        (shape((tokens, channels), f32), shape((peers, cuts, CUT), f32)),
        [VMEM] * 6,
        flops=2 * tokens * STATE * channels,
    )(entering, c_turned, base_0, carry_0, base_1, carry_1)
    summed = lax.all_to_all(squares, "chan", 0, 0, tiled=True)
    return call(
        norm_kernel,
        shape((tokens, channels), bf16),
        [VMEM] * 3,
        [pltpu.VMEM((tokens, channels), bf16), dma((4,))],
        out_specs=HBM,
    )(summed, norm_gain.reshape(1, channels), gated)


def solution(mesh):
    chan = mesh.shape["chan"]
    split = Mesh(mesh.devices.reshape(8, 4, 2, chan), (*SEQ, "chan"))
    placed = (
        P(SEQ, "chan"),
        P(SEQ, "chan"),
        P(SEQ, None),
        P(SEQ, None),
        P("chan", SEQ),
        P("chan", SEQ),
        P("chan"),
        P("chan"),
    )
    return jax.shard_map(
        per_device, mesh=split, in_specs=placed, out_specs=P(SEQ, "chan"), check_vma=False
    )
```

time: 65.2 us -> 60 us (0.920)
  blocking collectives: 37.2 us -> 17.1 us
  waiting for transfers between devices: 0.01 us -> 10.4 us
  starting transfers between devices: 11.6 us -> 16.1 us
    all_to_all x1 -> x0, blocking collectives: 20.2 us -> none  [per_device(): entering = lax.all_to_all(before, SEQ, 0, 0, tiled=True)]
    all_to_all x1, waiting for transfers between devices: 0.01 us -> 5.9 us  [per_device(): got = lax.all_to_all(message, SEQ, 0, 0, tiled=True)]
    all_to_all x0 -> x1, waiting for transfers between devices: none -> 4.51 us  [per_device(): entering = lax.all_to_all(before, SEQ, 0, 0, tiled=True)]
    all_to_all x0 -> x1, starting transfers between devices: none -> 4.44 us  [per_device(): entering = lax.all_to_all(before, SEQ, 0, 0, tiled=True)]
    pallas_call x4 -> x5, Pallas kernels: 15.1 us -> 15.1 us  [the longest x1 5.57 us: per_device(): call(late_kernel, local_shapes, [VMEM] * 2 + [SMEM] + [HBM] * 6, [*local_...]
  transfers between devices with their start and end apart: 1 -> 2, of which waited for: 0 -> 2; matrix products, arithmetic and copies ran while one was open for 0% -> 0% of each run, Pallas kernels for 16% -> 17%
where the time goes in v2:
time: 60 us; the launch traced here: 59.6 us
  blocking collectives  17.1 us (29%)
  starting transfers between devices  16.1 us (27%)
  Pallas kernels  16 us (27%)
  waiting for transfers between devices  10.4 us (17%)
    all_to_all x1, blocking collectives, per_device(): summed = lax.all_to_all(squares, 'chan', 0, 0, tiled=True)  17.1 us
    all_to_all x1, starting transfers between devices, per_device(): got = lax.all_to_all(message, SEQ, 0, 0, tiled=True)  11.6 us
    all_to_all x1, waiting for transfers between devices, per_device(): got = lax.all_to_all(message, SEQ, 0, 0, tiled=True)  5.9 us
    pallas_call x1, Pallas kernels, per_device(): call(late_kernel, local_shapes, [VMEM] * 2 + [SMEM] + [HBM] * 6, [*local_...  5.57 us
    pallas_call x1, Pallas kernels, per_device(): call(early_kernel, (*local_shapes, shape((STATE, channels), f32)), [SMEM]...  4.68 us
    all_to_all x1, waiting for transfers between devices, per_device(): entering = lax.all_to_all(before, SEQ, 0, 0, tiled=True)  4.51 us
    all_to_all x1, starting transfers between devices, per_device(): entering = lax.all_to_all(before, SEQ, 0, 0, tiled=True)  4.44 us
    pallas_call x1, Pallas kernels, per_device(): call(end_state_kernel, (shape((STATE, 1, channels + CUT), f32), part, *ne...  2.53 us
  transfers between devices with their start and end apart: 2, of which 2 were waited for; matrix products, arithmetic and copies ran while one was open for 0% of the time, Pallas kernels for 17%

profile of v2, /device:TPU:1, one launch (start us, length us, event | category | flops | bytes accessed | tf_op | source)
XLA Modules:
  0.0 59.6 jit_solution(1367399714682288712)
XLA Ops:
  0.0 2.5 %shard_map.82 = (f32[64,1,384]{2,1,0:T(1,128)}, bf16[1024,256]{1,0:T(8,128)(2,1)S(1)}, bf16[64,2048]{1,0:T(8,128)(2,1)S(1)}, bf16[64,2048]{1,0:T(8,128)(2,1)S(1)...) custom-call(bf16[2048,256]{1,0:T(8,128)(2,1)} %x_hbm.3, bf16[64,2048]{1,0:T(8,128)(2,1)} %bitcast.7, ...), custom_call_target="tpu_custom_call" | custom-call | flops 67108864 | bytes 4194304 | tf_op jit(solution)/shard_map/pallas_call | solution.py:374
  2.5 11.6 %all-to-all-start = ((f32[64,1,384]{2,1,0:T(1,128)}), f32[64,1,384]{2,1,0:T(1,128)S(1)}, u32[]{:S(2)}, u32[]{:S(2)}) async-start(f32[64,1,384]{2,1,0:T(1,128)} %get-tuple-element.20), calls=%async_computation | async-start | bytes 196608 | tf_op jit(solution)/shard_map/all_to_all | solution.py:381
  14.2 4.7 %shard_map.83 = (f32[1024,256]{1,0:T(8,128)S(1)}, bf16[1024,256]{1,0:T(8,128)(2,1)S(1)}, f32[64,256]{1,0:T(8,128)S(1)}) custom-call(f32[4]{0:T(128)} %skip_ref.3, bf16[1024,256]{1,0:T(8,128)(2,1)S(1)} %get-tuple-element.21.x_ref, bf16[64,2048]{1,0:T(8,128)(2,1)S(1)} %get-tuple-element.22.b_ref, bf16[64,2048]{1,0:T(8,128)(2,1)S(1)} %get-tuple-element.23.c_ref, ...), custom_call_target="tpu_custom_call" | custom-call | flops 5000000000 | bytes 4194304 | tf_op jit(solution)/shard_map/pallas_call | solution.py:382
  18.9 5.9 %all-to-all-done.got_ref = f32[64,1,384]{2,1,0:T(1,128)S(1)} async-done(((f32[64,1,384]{2,1,0:T(1,128)}), f32[64,1,384]{2,1,0:T(1,128)S(1)}, u32[]{:S(2)}, u32[]{:S(2)}) %all-to-all-start) | async-done | bytes 98336 | tf_op jit(solution)/shard_map/all_to_all | solution.py:381
  24.8 1.0 %shard_map.84 = (f32[64,1,256]{2,1,0:T(1,128)}, f32[8,128]{1,0:T(8,128)S(1)}) custom-call(f32[64,1,384]{2,1,0:T(1,128)S(1)} %all-to-all-done.got_ref, f32[64,256]{1,0:T(8,128)S(1)} %get-tuple-element.26._.state_in), custom_call_target="tpu_custom_call" | custom-call | flops 1000000 | bytes 4194304 | tf_op jit(solution)/shard_map/pallas_call | solution.py:389
  25.7 4.4 %all-to-all-start.1 = ((f32[64,1,256]{2,1,0:T(1,128)}), f32[64,1,256]{2,1,0:T(1,128)S(1)}, u32[]{:S(2)}, u32[]{:S(2)}) async-start(f32[64,1,256]{2,1,0:T(1,128)} %get-tuple-element.27), calls=%async_computation.1 | async-start | bytes 131072 | tf_op jit(solution)/shard_map/all_to_all | solution.py:395
  30.2 0.0 copy-start
  30.2 5.6 %shard_map.85 = (f32[1024,256]{1,0:T(8,128)S(1)}, bf16[1024,256]{1,0:T(8,128)(2,1)S(1)}) custom-call(f32[8,128]{1,0:T(8,128)S(1)} %get-tuple-element.30.flag_ref, f32[64,256]{1,0:T(8,128)S(1)} %get-tuple-element.26._.state_in, f32[4]{0:T(128)} %skip_ref.3, bf16[2048,256]{1,0:T(8,128)(2,1)} %x_hbm.3, bf16[64,2048]{1,0:T(8,128)(2,1)} %bitcast.8, ...), custom_call_target="tpu_custom_call" | custom-call | flops 5000000000 | bytes 4194304 | tf_op jit(solution)/shard_map/pallas_call | solution.py:396
  35.8 0.0 copy-start.1
  35.8 4.5 %all-to-all-done.1.got_ref = f32[64,1,256]{2,1,0:T(1,128)S(1)} async-done(((f32[64,1,256]{2,1,0:T(1,128)}), f32[64,1,256]{2,1,0:T(1,128)S(1)}, u32[]{:S(2)}, u32[]{:S(2)}) %all-to-all-start.1) | async-done | bytes 65568 | tf_op jit(solution)/shard_map/all_to_all | solution.py:395
  40.3 0.0 copy-done
  40.3 1.0 %shard_map.86 = (f32[2048,256]{1,0:T(8,128)S(1)}, f32[8,16,128]{2,1,0:T(8,128)S(1)}) custom-call(f32[64,1,256]{2,1,0:T(1,128)S(1)} %all-to-all-done.1.got_ref, bf16[64,2048]{1,0:T(8,128)(2,1)S(1)} %bitcast.5, f32[1024,256]{1,0:T(8,128)S(1)} %get-tuple-element.28.refs_0_, bf16[1024,256]{1,0:T(8,128)(2,1)S(1)} %get-tuple-element.29.refs_1_, ...), custom_call_target="tpu_custom_call" | custom-call | flops 67108864 | bytes 4194304 | tf_op jit(solution)/shard_map/pallas_call | solution.py:407
  41.3 17.1 %all_to_all.15.got_ref = f32[8,16,128]{2,1,0:T(8,128)S(1)} all-to-all(f32[8,16,128]{2,1,0:T(8,128)S(1)} %get-tuple-element.33), channel_id=1, replica_groups=mesh['seq_0'=8,'seq_1'=4,'seq_2'=2,'chan'=8] {'chan'}, dimensions={0} | all-to-all | bytes 131072 | tf_op jit(solution)/shard_map/all_to_all | solution.py:413
  58.3 0.0 copy-done.1
  58.3 1.3 %shard_map.87 = bf16[2048,256]{1,0:T(8,128)(2,1)} custom-call(f32[8,16,128]{2,1,0:T(8,128)S(1)} %all_to_all.15.got_ref, f32[1,256]{1,0:T(1,128)S(1)} %bitcast.6, f32[2048,256]{1,0:T(8,128)S(1)} %get-tuple-element.34.gated_ref), custom_call_target="tpu_custom_call" | custom-call | flops 1000000 | bytes 4194304 | tf_op jit(solution)/shard_map/pallas_call | solution.py:414
Async XLA Ops:
  2.5 22.2 %all-to-all-start = ((f32[64,1,384]{2,1,0:T(1,128)}), f32[64,1,384]{2,1,0:T(1,128)S(1)}, u32[]{:S(2)}, u32[]{:S(2)}) async-start(f32[64,1,384]{2,1,0:T(1,128)} %get-tuple-element.20), calls=%async_computation | async-start | bytes 196608 | tf_op jit(solution)/shard_map/all_to_all | solution.py:381
  25.7 14.6 %all-to-all-start.1 = ((f32[64,1,256]{2,1,0:T(1,128)}), f32[64,1,256]{2,1,0:T(1,128)S(1)}, u32[]{:S(2)}, u32[]{:S(2)}) async-start(f32[64,1,256]{2,1,0:T(1,128)} %get-tuple-element.27), calls=%async_computation.1 | async-start | bytes 131072 | tf_op jit(solution)/shard_map/all_to_all | solution.py:395
  30.2 10.1 %copy-start = (bf16[2048,64]{0,1:T(8,128)(2,1)S(1)}, bf16[2048,64]{0,1:T(8,128)(2,1)}, u32[]{:S(2)}) copy-start(bf16[2048,64]{0,1:T(8,128)(2,1)} %param.11) | copy-start | bytes 786436
  35.8 22.6 %copy-start.1 = (f32[256]{0:T(256)S(1)}, f32[256]{0:T(256)}, u32[]{:S(2)}) copy-start(f32[256]{0:T(256)} %param.15) | copy-start | bytes 3076

commit v3 on v2

--- a/solution.py
+++ b/solution.py
@@ -5,18 +5,18 @@
 from jax import lax
 from jax.experimental import pallas as pl
 from jax.experimental.pallas import tpu as pltpu
-from jax.sharding import Mesh
 from jax.sharding import PartitionSpec as P
 
 CH = 2048
 HEAD = 64
 STATE = 64
-SEQ = ("seq_0", "seq_1", "seq_2")
+SEQ = "seq"
 CUT = 128
 EPSILON = 1e-05
 LOG2E = 1.4426950408889634
 MIB = 1024 * 1024
 UNROLL = 4
+FIRST = {"seq": 45, "chan": 5}
 
 f32 = jnp.float32
 bf16 = jnp.bfloat16
@@ -120,7 +120,7 @@
     copies[5].wait()
 
 
-def scan_kernel(heads, got_ref, _, out_ref, flag_ref, state_ref, decay_ref):
+def scan_kernel(heads, first, got_ref, _, out_ref, flag_ref, state_ref, decay_ref):
     flag_ref[...] = jnp.zeros_like(flag_ref)
     count = got_ref.shape[0]
     width = heads * HEAD
@@ -130,8 +130,9 @@
     decay_ref[...] = exact(got_ref[:, 0, width:], spread)
     state = jnp.zeros((1, width), f32)
     for k in range(count):
-        out_ref[k] = state
-        state = decay_ref[k : k + 1, :] * state + state_ref[k : k + 1, :]
+        at = (k - first) % count
+        out_ref[at] = state
+        state = decay_ref[at : at + 1, :] * state + state_ref[at : at + 1, :]
 
 
 def tile_copies(skipped, pairs, sems):
@@ -345,6 +346,12 @@
     )
 
 
+def exchange(v, axis):
+    size, first = lax.axis_size(axis), FIRST[axis]
+    places = [[(first + k) % size for k in range(size)]]
+    return lax.all_to_all(v, axis, 0, 0, axis_index_groups=places, tiled=True)
+
+
 def per_device(x_in, gate_in, b_in, c_in, step_size, log_keep, skip_gain, norm_gain):
     tokens, channels = x_in.shape
     heads = step_size.shape[0]
@@ -378,7 +385,7 @@
         [half_wide, rows, pltpu.VMEM((heads * STATE, tokens), bf16), dma((6,))],
         flops=2 * tokens * STATE * channels,
     )(x_in, b_turned, c_far, step_size, log_keep)
-    got = lax.all_to_all(message, SEQ, 0, 0, tiled=True)
+    got = exchange(message, SEQ)
     base_0, carry_0, state = call(
         early_kernel,
         (*local_shapes, shape((STATE, channels), f32)),
@@ -387,12 +394,12 @@
         flops=int(5e9),
     )(skip_gain, x_near, *near, gate_in)
     before, flag = call(
-        functools.partial(scan_kernel, heads),
+        functools.partial(scan_kernel, heads, FIRST["seq"]),
         (shape((STATE, 1, channels), f32), shape((8, CUT), f32)),
         [VMEM] * 2,
         [row, row],
     )(got, state)
-    entering = lax.all_to_all(before, SEQ, 0, 0, tiled=True)
+    entering = exchange(before, SEQ)
     base_1, carry_1 = call(
         late_kernel,
         local_shapes,
@@ -410,7 +417,7 @@
         [VMEM] * 6,
         flops=2 * tokens * STATE * channels,
     )(entering, c_turned, base_0, carry_0, base_1, carry_1)
-    summed = lax.all_to_all(squares, "chan", 0, 0, tiled=True)
+    summed = exchange(squares, "chan")
     return call(
         norm_kernel,
         shape((tokens, channels), bf16),
@@ -421,8 +428,6 @@
 
 
 def solution(mesh):
-    chan = mesh.shape["chan"]
-    split = Mesh(mesh.devices.reshape(8, 4, 2, chan), (*SEQ, "chan"))
     placed = (
         P(SEQ, "chan"),
         P(SEQ, "chan"),
@@ -434,5 +439,5 @@
         P("chan"),
     )
     return jax.shard_map(
-        per_device, mesh=split, in_specs=placed, out_specs=P(SEQ, "chan"), check_vma=False
-    )
+        per_device, mesh=mesh, in_specs=placed, out_specs=P(SEQ, "chan"), check_vma=False
+    )

time: 60 us -> 53.7 us (0.90)
  waiting for transfers between devices: 10.4 us -> 0.01 us
  starting transfers between devices: 16.1 us -> 25.4 us
  blocking collectives: 17.1 us -> 11.8 us
    all_to_all x2, waiting for transfers between devices: 10.4 us -> 0.01 us  [exchange(): return lax.all_to_all(v, axis, 0, 0, axis_index_groups=places, tiled=True)]
    all_to_all x2, starting transfers between devices: 16.1 us -> 25.4 us  [exchange(): return lax.all_to_all(v, axis, 0, 0, axis_index_groups=places, tiled=True)]
    all_to_all x1, blocking collectives: 17.1 us -> 11.8 us  [exchange(): return lax.all_to_all(v, axis, 0, 0, axis_index_groups=places, tiled=True)]
  transfers between devices with their start and end apart: 2 -> 2, of which waited for: 2 -> 0; matrix products, arithmetic and copies ran while one was open for 0% -> 0% of each run, Pallas kernels for 17% -> 19%
where the time goes in v3:
time: 53.7 us; the launch traced here: 53.4 us
  starting transfers between devices  25.4 us (47%)
  Pallas kernels  16 us (30%)
  blocking collectives  11.8 us (22%)
    all_to_all x2, starting transfers between devices, exchange(): return lax.all_to_all(v, axis, 0, 0, axis_index_groups=places, tiled=True)  25.4 us
    all_to_all x1, blocking collectives, exchange(): return lax.all_to_all(v, axis, 0, 0, axis_index_groups=places, tiled=True)  11.8 us
    pallas_call x1, Pallas kernels, per_device(): call(late_kernel, local_shapes, [VMEM] * 2 + [SMEM] + [HBM] * 6, [*local_...  5.57 us
    pallas_call x1, Pallas kernels, per_device(): call(early_kernel, (*local_shapes, shape((STATE, channels), f32)), [SMEM]...  4.68 us
    pallas_call x1, Pallas kernels, per_device(): call(end_state_kernel, (shape((STATE, 1, channels + CUT), f32), part, *ne...  2.53 us
    pallas_call x1, Pallas kernels, per_device(): call(norm_kernel, shape((tokens, channels), bf16), [VMEM] * 3, [pltpu.VME...  1.31 us
  transfers between devices with their start and end apart: 2, of which 0 were waited for; matrix products, arithmetic and copies ran while one was open for 0% of the time, Pallas kernels for 19%

profile of v3, /device:TPU:1, one launch (start us, length us, event | category | flops | bytes accessed | tf_op | source)
XLA Modules:
  0.0 53.4 jit_solution(6561938055561113986)
XLA Ops:
  0.0 2.5 %shard_map.82 = (f32[64,1,384]{2,1,0:T(1,128)}, bf16[1024,256]{1,0:T(8,128)(2,1)S(1)}, bf16[64,2048]{1,0:T(8,128)(2,1)S(1)}, bf16[64,2048]{1,0:T(8,128)(2,1)S(1)...) custom-call(bf16[2048,256]{1,0:T(8,128)(2,1)} %x_hbm.3, bf16[64,2048]{1,0:T(8,128)(2,1)} %bitcast.7, ...), custom_call_target="tpu_custom_call" | custom-call | flops 67108864 | bytes 4194304 | tf_op jit(solution)/shard_map/pallas_call | solution.py:381
  2.5 15.5 %all-to-all-start = ((f32[64,1,384]{2,1,0:T(1,128)}), f32[64,1,384]{2,1,0:T(1,128)S(1)}, u32[]{:S(2)}, u32[]{:S(2)}) async-start(f32[64,1,384]{2,1,0:T(1,128)} %get-tuple-element.20), calls=%async_computation | async-start | bytes 196608 | tf_op jit(solution)/shard_map/all_to_all | solution.py:352
  18.0 4.7 %shard_map.83 = (f32[1024,256]{1,0:T(8,128)S(1)}, bf16[1024,256]{1,0:T(8,128)(2,1)S(1)}, f32[64,256]{1,0:T(8,128)S(1)}) custom-call(f32[4]{0:T(128)} %skip_ref.3, bf16[1024,256]{1,0:T(8,128)(2,1)S(1)} %get-tuple-element.21.x_ref, bf16[64,2048]{1,0:T(8,128)(2,1)S(1)} %get-tuple-element.22.b_ref, bf16[64,2048]{1,0:T(8,128)(2,1)S(1)} %get-tuple-element.23.c_ref, ...), custom_call_target="tpu_custom_call" | custom-call | flops 5000000000 | bytes 4194304 | tf_op jit(solution)/shard_map/pallas_call | solution.py:389
  22.7 0.0 all-to-all-done.got_ref
  22.7 1.0 %shard_map.84 = (f32[64,1,256]{2,1,0:T(1,128)}, f32[8,128]{1,0:T(8,128)S(1)}) custom-call(f32[64,1,384]{2,1,0:T(1,128)S(1)} %all-to-all-done.got_ref, f32[64,256]{1,0:T(8,128)S(1)} %get-tuple-element.26._.state_in), custom_call_target="tpu_custom_call" | custom-call | flops 1000000 | bytes 4194304 | tf_op jit(solution)/shard_map/pallas_call | solution.py:396
  23.7 10.0 %all-to-all-start.1 = ((f32[64,1,256]{2,1,0:T(1,128)}), f32[64,1,256]{2,1,0:T(1,128)S(1)}, u32[]{:S(2)}, u32[]{:S(2)}) async-start(f32[64,1,256]{2,1,0:T(1,128)} %get-tuple-element.27), calls=%async_computation.1 | async-start | bytes 131072 | tf_op jit(solution)/shard_map/all_to_all | solution.py:352
  33.6 0.0 copy-start
  33.7 5.6 %shard_map.85 = (f32[1024,256]{1,0:T(8,128)S(1)}, bf16[1024,256]{1,0:T(8,128)(2,1)S(1)}) custom-call(f32[8,128]{1,0:T(8,128)S(1)} %get-tuple-element.30.flag_ref, f32[64,256]{1,0:T(8,128)S(1)} %get-tuple-element.26._.state_in, f32[4]{0:T(128)} %skip_ref.3, bf16[2048,256]{1,0:T(8,128)(2,1)} %x_hbm.3, bf16[64,2048]{1,0:T(8,128)(2,1)} %bitcast.8, ...), custom_call_target="tpu_custom_call" | custom-call | flops 5000000000 | bytes 4194304 | tf_op jit(solution)/shard_map/pallas_call | solution.py:403
  39.2 0.0 copy-start.1
  39.2 0.0 all-to-all-done.1.got_ref
  39.3 0.0 copy-done
  39.3 1.0 %shard_map.86 = (f32[2048,256]{1,0:T(8,128)S(1)}, f32[8,16,128]{2,1,0:T(8,128)S(1)}) custom-call(f32[64,1,256]{2,1,0:T(1,128)S(1)} %all-to-all-done.1.got_ref, bf16[64,2048]{1,0:T(8,128)(2,1)S(1)} %bitcast.5, f32[1024,256]{1,0:T(8,128)S(1)} %get-tuple-element.28.refs_0_, bf16[1024,256]{1,0:T(8,128)(2,1)S(1)} %get-tuple-element.29.refs_1_, ...), custom_call_target="tpu_custom_call" | custom-call | flops 67108864 | bytes 4194304 | tf_op jit(solution)/shard_map/pallas_call | solution.py:414
  40.2 11.8 %all_to_all.15.got_ref = f32[8,16,128]{2,1,0:T(8,128)S(1)} all-to-all(f32[8,16,128]{2,1,0:T(8,128)S(1)} %get-tuple-element.33), channel_id=1, replica_groups={{5,6,7,0,1,2,3,4},{13,14,15,8,9,10,11,12},{21,22,23,16,17,18,19,20},{29..., dimensions={0} | all-to-all | bytes 131072 | tf_op jit(solution)/shard_map/all_to_all | solution.py:352
  52.1 0.0 copy-done.1
  52.1 1.3 %shard_map.87 = bf16[2048,256]{1,0:T(8,128)(2,1)} custom-call(f32[8,16,128]{2,1,0:T(8,128)S(1)} %all_to_all.15.got_ref, f32[1,256]{1,0:T(1,128)S(1)} %bitcast.6, f32[2048,256]{1,0:T(8,128)S(1)} %get-tuple-element.34.gated_ref), custom_call_target="tpu_custom_call" | custom-call | flops 1000000 | bytes 4194304 | tf_op jit(solution)/shard_map/pallas_call | solution.py:421
Async XLA Ops:
  2.5 20.2 %all-to-all-start = ((f32[64,1,384]{2,1,0:T(1,128)}), f32[64,1,384]{2,1,0:T(1,128)S(1)}, u32[]{:S(2)}, u32[]{:S(2)}) async-start(f32[64,1,384]{2,1,0:T(1,128)} %get-tuple-element.20), calls=%async_computation | async-start | bytes 196608 | tf_op jit(solution)/shard_map/all_to_all | solution.py:352
  23.7 15.6 %all-to-all-start.1 = ((f32[64,1,256]{2,1,0:T(1,128)}), f32[64,1,256]{2,1,0:T(1,128)S(1)}, u32[]{:S(2)}, u32[]{:S(2)}) async-start(f32[64,1,256]{2,1,0:T(1,128)} %get-tuple-element.27), calls=%async_computation.1 | async-start | bytes 131072 | tf_op jit(solution)/shard_map/all_to_all | solution.py:352
  33.6 5.6 %copy-start = (bf16[2048,64]{0,1:T(8,128)(2,1)S(1)}, bf16[2048,64]{0,1:T(8,128)(2,1)}, u32[]{:S(2)}) copy-start(bf16[2048,64]{0,1:T(8,128)(2,1)} %param.11) | copy-start | bytes 786436
  39.2 12.8 %copy-start.1 = (f32[256]{0:T(256)S(1)}, f32[256]{0:T(256)}, u32[]{:S(2)}) copy-start(f32[256]{0:T(256)} %param.15) | copy-start | bytes 3076

commit v4 on v3

--- a/solution.py
+++ b/solution.py
@@ -66,7 +66,7 @@
 def end_state_kernel(
     x_hbm, b_hbm, c_hbm, step_hbm, keep_hbm,
     out_ref, x_ref, b_ref, c_ref, step_ref, keep_ref,
-    x_rest, factor, lhs, sems,
+    x_rest, factor, sems,
 ):
     half = x_ref.shape[0]
     copies = [
@@ -94,7 +94,8 @@
     count = heads * cuts
     row, col = iota((count, count), 0), iota((count, count), 1)
     same = row % heads == col % heads
-    later = exact(jnp.where(same & (col // heads > row // heads), 1.0, 0.0), total)
+    mask = jnp.where(same & (col // heads > row // heads), 1.0, 0.0).astype(bf16)
+    later = sum(dot(mask, piece.astype(bf16)) for piece in reversed(split3(total)))
     decay = jnp.exp(later[:heads] + total[:heads])
     lane = iota((1, CUT), 1) // (CUT // heads)
     decays = jnp.zeros((1, CUT), f32)
@@ -103,36 +104,64 @@
     copies[1].wait()
     factor[...] = jnp.exp(after + later) * by_cut(step_ref)
     copies[2].wait()
-    for k in range(cuts):
-        part = b_ref[:, k * CUT : (k + 1) * CUT].astype(f32)
-        for h in range(heads):
-            scaled = part * factor[k * heads + h : k * heads + h + 1, :]
-            lhs[h * STATE : (h + 1) * STATE, k * CUT : (k + 1) * CUT] = scaled.astype(bf16)
-    copies[3].wait()
-    copies[4].wait()
     pairs = heads // 2
+    both = [jnp.zeros((2 * STATE, CUT), f32)] * pairs
+    for k in range(0, cuts, 2):
+        at = k * CUT
+        near = x_ref if at < half else x_rest
+        if at % half == 0:
+            copies[3 + at // half].wait()
+        part = b_ref[:, at : at + 2 * CUT].astype(f32)
+        for pair in range(pairs):
+            lhs = []
+            for h in range(2 * pair, 2 * pair + 2):
+                rows = [factor[(k + i) * heads + h : (k + i) * heads + h + 1, :] for i in range(2)]
+                lhs.append((part * jnp.concatenate(rows, axis=1)).astype(bf16))
+            x = near[at % half : at % half + 2 * CUT, pair * CUT : (pair + 1) * CUT]
+            both[pair] = both[pair] + dot(jnp.concatenate(lhs, axis=0), x)
     for pair in range(pairs):
         lanes = slice(pair * CUT, (pair + 1) * CUT)
-        rows = slice(pair * 2 * STATE, (pair + 1) * 2 * STATE)
-        both = dot(lhs[rows, :half], x_ref[:, lanes]) + dot(lhs[rows, half:], x_rest[:, lanes])
-        out_ref[:, 0, lanes] = two_heads(both[:STATE], both[STATE:])
+        out_ref[:, 0, lanes] = two_heads(both[pair][:STATE], both[pair][STATE:])
     out_ref[:, 0, pairs * CUT :] = jnp.broadcast_to(decays, (STATE, CUT))
     copies[5].wait()
 
 
-def scan_kernel(heads, first, got_ref, _, out_ref, flag_ref, state_ref, decay_ref):
+def scan_kernel(heads, first, got_ref, _, out_ref, flag_ref, *refs):
     flag_ref[...] = jnp.zeros_like(flag_ref)
     count = got_ref.shape[0]
     width = heads * HEAD
-    state_ref[...] = got_ref[:, 0, :width]
+    seam = count - first
+
+    def rolled(lanes):
+        return jnp.concatenate([got_ref[seam:, 0, lanes], got_ref[:seam, 0, lanes]], axis=0)
+
     row, col = iota((CUT, width), 0), iota((CUT, width), 1)
     spread = jnp.where(row == col // HEAD * (CUT // heads), 1.0, 0.0)
-    decay_ref[...] = exact(got_ref[:, 0, width:], spread)
-    state = jnp.zeros((1, width), f32)
-    for k in range(count):
-        at = (k - first) % count
-        out_ref[at] = state
-        state = decay_ref[at : at + 1, :] * state + state_ref[at : at + 1, :]
+    all_decays = sum_of_pieces(rolled(slice(width, width + CUT)), spread)
+    groups = 8
+    steps = count // groups
+    for part in range(width // CUT):
+        lanes = slice(part * CUT, (part + 1) * CUT)
+        state_ref, decay_ref = refs[2 * part : 2 * part + 2]
+        state_ref[...] = rolled(lanes)
+        decay_ref[...] = all_decays[:, lanes]
+        states, decays = [], []
+        for j in range(steps):
+            at = pl.ds(j, groups, stride=steps)
+            state, decay = state_ref[at, :], decay_ref[at, :]
+            if j:
+                state, decay = state + decay * states[-1], decay * decays[-1]
+            states.append(state)
+            decays.append(decay)
+        carries = [jnp.zeros((1, CUT), f32)]
+        for g in range(groups - 1):
+            carries.append(decays[-1][g : g + 1] * carries[-1] + states[-1][g : g + 1])
+        carry = jnp.concatenate(carries, axis=0)
+        for j in range(steps):
+            before = states[j - 1] + decays[j - 1] * carry if j else carry
+            state_ref[pl.ds(j, groups, stride=steps), :] = before
+        out_ref[seam:, 0, lanes] = state_ref[:first, :]
+        out_ref[:seam, 0, lanes] = state_ref[first:, :]
 
 
 def tile_copies(skipped, pairs, sems):
@@ -230,7 +259,6 @@
         at = pl.ds(pl.multiple_of(k * CUT, CUT), CUT)
         far = pl.ds(pl.multiple_of((skipped + k) * CUT, CUT), CUT)
         first = (skipped + k) * heads
-        wait_tile(k)
         b = b_ref[:, far]
         c = jnp.transpose(c_ref[:, far])
         growths = jnp.transpose(left[k])
@@ -270,6 +298,8 @@
         return 0
 
     wait_rest()
+    for k in range(mine):
+        wait_tile(k)
     lax.fori_loop(0, mine, one_cut, 0, unroll=UNROLL)
 
 
@@ -320,9 +350,9 @@
         rows = [piece[k : k + 1] for piece in pieces] + [jnp.zeros((5, CUT), f32)]
         factor = dot(jnp.transpose(jnp.concatenate(rows, axis=0)).astype(bf16), ones)
         out_ref[at, :] = (gated_ref[at, :] * factor * gain).astype(bf16)
-        if k % 4 == 3:
-            four = pl.ds((k - 3) * CUT, 4 * CUT)
-            copy = pltpu.make_async_copy(out_ref.at[four], out_hbm.at[four], sems.at[k // 4])
+        if k % 2 == 1:
+            two = pl.ds((k - 1) * CUT, 2 * CUT)
+            copy = pltpu.make_async_copy(out_ref.at[two], out_hbm.at[two], sems.at[k // 2])
             copy.start()
             copies.append(copy)
     for copy in copies:
@@ -382,7 +412,7 @@
         end_state_kernel,
         (shape((STATE, 1, channels + CUT), f32), part, *near_shapes),
         [HBM] * 5,
-        [half_wide, rows, pltpu.VMEM((heads * STATE, tokens), bf16), dma((6,))],
+        [half_wide, rows, dma((6,))],
         flops=2 * tokens * STATE * channels,
     )(x_in, b_turned, c_far, step_size, log_keep)
     got = exchange(message, SEQ)
@@ -397,7 +427,7 @@
         functools.partial(scan_kernel, heads, FIRST["seq"]),
         (shape((STATE, 1, channels), f32), shape((8, CUT), f32)),
         [VMEM] * 2,
-        [row, row],
+        [pltpu.VMEM((STATE, CUT), f32)] * (2 * channels // CUT),
     )(got, state)
     entering = exchange(before, SEQ)
     base_1, carry_1 = call(
@@ -422,7 +452,7 @@
         norm_kernel,
         shape((tokens, channels), bf16),
         [VMEM] * 3,
-        [pltpu.VMEM((tokens, channels), bf16), dma((4,))],
+        [pltpu.VMEM((tokens, channels), bf16), dma((cuts // 2,))],
         out_specs=HBM,
     )(summed, norm_gain.reshape(1, channels), gated)
 

time: 53.7 us -> 52.6 us (0.980)
  Pallas kernels: 16 us -> 14.7 us
    pallas_call x1, Pallas kernels: 5.57 us -> 4.81 us  [per_device(): call(late_kernel, local_shapes, [VMEM] * 2 + [SMEM] + [HBM] * 6, [*local_...]
  transfers between devices with their start and end apart: 2 -> 2, of which waited for: 0 -> 1; matrix products, arithmetic and copies ran while one was open for 0% -> 0% of each run, Pallas kernels for 19% -> 17%
where the time goes in v4:
time: 52.6 us; the launch traced here: 52.2 us
  starting transfers between devices  25.5 us (48%)
  Pallas kernels  14.7 us (28%)
  blocking collectives  11.8 us (22%)
    all_to_all x2, starting transfers between devices, exchange(): return lax.all_to_all(v, axis, 0, 0, axis_index_groups=places, tiled=True)  25.5 us
    all_to_all x1, blocking collectives, exchange(): return lax.all_to_all(v, axis, 0, 0, axis_index_groups=places, tiled=True)  11.8 us
    pallas_call x1, Pallas kernels, per_device(): call(late_kernel, local_shapes, [VMEM] * 2 + [SMEM] + [HBM] * 6, [*local_...  4.81 us
    pallas_call x1, Pallas kernels, per_device(): call(early_kernel, (*local_shapes, shape((STATE, channels), f32)), [SMEM]...  4.21 us
    pallas_call x1, Pallas kernels, per_device(): call(end_state_kernel, (shape((STATE, 1, channels + CUT), f32), part, *ne...  2.48 us
    pallas_call x1, Pallas kernels, per_device(): call(norm_kernel, shape((tokens, channels), bf16), [VMEM] * 3, [pltpu.VME...  1.3 us
  transfers between devices with their start and end apart: 2, of which 1 were waited for; matrix products, arithmetic and copies ran while one was open for 0% of the time, Pallas kernels for 17%

profile of v4, /device:TPU:1, one launch (start us, length us, event | category | flops | bytes accessed | tf_op | source)
XLA Modules:
  0.0 52.2 jit_solution(8209780981571949826)
XLA Ops:
  0.0 2.5 %shard_map.82 = (f32[64,1,384]{2,1,0:T(1,128)}, bf16[1024,256]{1,0:T(8,128)(2,1)S(1)}, bf16[64,2048]{1,0:T(8,128)(2,1)S(1)}, bf16[64,2048]{1,0:T(8,128)(2,1)S(1)...) custom-call(bf16[2048,256]{1,0:T(8,128)(2,1)} %x_hbm.3, bf16[64,2048]{1,0:T(8,128)(2,1)} %bitcast.7, ...), custom_call_target="tpu_custom_call" | custom-call | flops 67108864 | bytes 4194304 | tf_op jit(solution)/shard_map/pallas_call | solution.py:411
  2.5 15.5 %all-to-all-start = ((f32[64,1,384]{2,1,0:T(1,128)}), f32[64,1,384]{2,1,0:T(1,128)S(1)}, u32[]{:S(2)}, u32[]{:S(2)}) async-start(f32[64,1,384]{2,1,0:T(1,128)} %get-tuple-element.20), calls=%async_computation | async-start | bytes 196608 | tf_op jit(solution)/shard_map/all_to_all | solution.py:382
  18.0 4.2 %shard_map.83 = (f32[1024,256]{1,0:T(8,128)S(1)}, bf16[1024,256]{1,0:T(8,128)(2,1)S(1)}, f32[64,256]{1,0:T(8,128)S(1)}) custom-call(f32[4]{0:T(128)} %skip_ref.3, bf16[1024,256]{1,0:T(8,128)(2,1)S(1)} %get-tuple-element.21.x_ref, bf16[64,2048]{1,0:T(8,128)(2,1)S(1)} %get-tuple-element.22.b_ref, bf16[64,2048]{1,0:T(8,128)(2,1)S(1)} %get-tuple-element.23.c_ref, ...), custom_call_target="tpu_custom_call" | custom-call | flops 5000000000 | bytes 4194304 | tf_op jit(solution)/shard_map/pallas_call | solution.py:419
  22.2 0.2 all-to-all-done.got_ref
  22.4 0.9 %shard_map.84 = (f32[64,1,256]{2,1,0:T(1,128)}, f32[8,128]{1,0:T(8,128)S(1)}) custom-call(f32[64,1,384]{2,1,0:T(1,128)S(1)} %all-to-all-done.got_ref, f32[64,256]{1,0:T(8,128)S(1)} %get-tuple-element.26._.state_in), custom_call_target="tpu_custom_call" | custom-call | flops 1000000 | bytes 4194304 | tf_op jit(solution)/shard_map/pallas_call | solution.py:426
  23.3 10.0 %all-to-all-start.1 = ((f32[64,1,256]{2,1,0:T(1,128)}), f32[64,1,256]{2,1,0:T(1,128)S(1)}, u32[]{:S(2)}, u32[]{:S(2)}) async-start(f32[64,1,256]{2,1,0:T(1,128)} %get-tuple-element.27), calls=%async_computation.1 | async-start | bytes 131072 | tf_op jit(solution)/shard_map/all_to_all | solution.py:382
  33.3 0.0 copy-start
  33.3 4.8 %shard_map.85 = (f32[1024,256]{1,0:T(8,128)S(1)}, bf16[1024,256]{1,0:T(8,128)(2,1)S(1)}) custom-call(f32[8,128]{1,0:T(8,128)S(1)} %get-tuple-element.30.flag_ref, f32[64,256]{1,0:T(8,128)S(1)} %get-tuple-element.26._.state_in, f32[4]{0:T(128)} %skip_ref.3, bf16[2048,256]{1,0:T(8,128)(2,1)} %x_hbm.3, bf16[64,2048]{1,0:T(8,128)(2,1)} %bitcast.8, ...), custom_call_target="tpu_custom_call" | custom-call | flops 5000000000 | bytes 4194304 | tf_op jit(solution)/shard_map/pallas_call | solution.py:433
  38.1 0.0 copy-start.1
  38.1 0.0 all-to-all-done.1.got_ref
  38.1 0.0 copy-done
  38.1 1.0 %shard_map.86 = (f32[2048,256]{1,0:T(8,128)S(1)}, f32[8,16,128]{2,1,0:T(8,128)S(1)}) custom-call(f32[64,1,256]{2,1,0:T(1,128)S(1)} %all-to-all-done.1.got_ref, bf16[64,2048]{1,0:T(8,128)(2,1)S(1)} %bitcast.5, f32[1024,256]{1,0:T(8,128)S(1)} %get-tuple-element.28.refs_0_, bf16[1024,256]{1,0:T(8,128)(2,1)S(1)} %get-tuple-element.29.refs_1_, ...), custom_call_target="tpu_custom_call" | custom-call | flops 67108864 | bytes 4194304 | tf_op jit(solution)/shard_map/pallas_call | solution.py:444
  39.1 11.8 %all_to_all.15.got_ref = f32[8,16,128]{2,1,0:T(8,128)S(1)} all-to-all(f32[8,16,128]{2,1,0:T(8,128)S(1)} %get-tuple-element.33), channel_id=1, replica_groups={{5,6,7,0,1,2,3,4},{13,14,15,8,9,10,11,12},{21,22,23,16,17,18,19,20},{29..., dimensions={0} | all-to-all | bytes 131072 | tf_op jit(solution)/shard_map/all_to_all | solution.py:382
  50.9 0.0 copy-done.1
  50.9 1.3 %shard_map.87 = bf16[2048,256]{1,0:T(8,128)(2,1)} custom-call(f32[8,16,128]{2,1,0:T(8,128)S(1)} %all_to_all.15.got_ref, f32[1,256]{1,0:T(1,128)S(1)} %bitcast.6, f32[2048,256]{1,0:T(8,128)S(1)} %get-tuple-element.34.gated_ref), custom_call_target="tpu_custom_call" | custom-call | flops 1000000 | bytes 4194304 | tf_op jit(solution)/shard_map/pallas_call | solution.py:451
Async XLA Ops:
  2.5 19.9 %all-to-all-start = ((f32[64,1,384]{2,1,0:T(1,128)}), f32[64,1,384]{2,1,0:T(1,128)S(1)}, u32[]{:S(2)}, u32[]{:S(2)}) async-start(f32[64,1,384]{2,1,0:T(1,128)} %get-tuple-element.20), calls=%async_computation | async-start | bytes 196608 | tf_op jit(solution)/shard_map/all_to_all | solution.py:382
  23.3 14.9 %all-to-all-start.1 = ((f32[64,1,256]{2,1,0:T(1,128)}), f32[64,1,256]{2,1,0:T(1,128)S(1)}, u32[]{:S(2)}, u32[]{:S(2)}) async-start(f32[64,1,256]{2,1,0:T(1,128)} %get-tuple-element.27), calls=%async_computation.1 | async-start | bytes 131072 | tf_op jit(solution)/shard_map/all_to_all | solution.py:382
  33.3 4.9 %copy-start = (bf16[2048,64]{0,1:T(8,128)(2,1)S(1)}, bf16[2048,64]{0,1:T(8,128)(2,1)}, u32[]{:S(2)}) copy-start(bf16[2048,64]{0,1:T(8,128)(2,1)} %param.11) | copy-start | bytes 786436
  38.1 12.8 %copy-start.1 = (f32[256]{0:T(256)S(1)}, f32[256]{0:T(256)}, u32[]{:S(2)}) copy-start(f32[256]{0:T(256)} %param.15) | copy-start | bytes 3076

commit v5 on v4

--- a/solution.py
+++ b/solution.py
@@ -16,7 +16,7 @@
 LOG2E = 1.4426950408889634
 MIB = 1024 * 1024
 UNROLL = 4
-FIRST = {"seq": 45, "chan": 5}
+FIRST = {"seq": 47, "chan": 5}
 
 f32 = jnp.float32
 bf16 = jnp.bfloat16
@@ -64,8 +64,8 @@
 
 
 def end_state_kernel(
-    x_hbm, b_hbm, c_hbm, step_hbm, keep_hbm,
-    out_ref, x_ref, b_ref, c_ref, step_ref, keep_ref,
+    x_hbm, gate_hbm, b_hbm, c_hbm, step_hbm, keep_hbm,
+    out_ref, x_ref, gate_ref, b_ref, c_ref, step_ref, keep_ref,
     x_rest, factor, sems,
 ):
     half = x_ref.shape[0]
@@ -79,6 +79,7 @@
                 (x_hbm.at[pl.ds(0, half)], x_ref),
                 (x_hbm.at[pl.ds(half, half)], x_rest),
                 (c_hbm, c_ref),
+                (gate_hbm.at[pl.ds(0, half)], gate_ref),
             )
         )
     ]
@@ -124,6 +125,7 @@
         out_ref[:, 0, lanes] = two_heads(both[pair][:STATE], both[pair][STATE:])
     out_ref[:, 0, pairs * CUT :] = jnp.broadcast_to(decays, (STATE, CUT))
     copies[5].wait()
+    copies[6].wait()
 
 
 def scan_kernel(heads, first, got_ref, _, out_ref, flag_ref, *refs):
@@ -164,71 +166,53 @@
         out_ref[:seam, 0, lanes] = state_ref[first:, :]
 
 
-def tile_copies(skipped, pairs, sems):
-    def copies(k):
-        source = pl.ds(pl.multiple_of((skipped + k) * CUT, CUT), CUT)
-        at = pl.ds(pl.multiple_of(k * CUT, CUT), CUT)
-        return [
-            pltpu.make_async_copy(far.at[source], near.at[at], sems.at[i, k])
-            for i, (far, near) in enumerate(pairs)
-        ]
-
-    def wait(k):
-        for copy in copies(k):
-            copy.wait()
-
-    for k in range(pairs[0][1].shape[0] // CUT):
-        for copy in copies(k):
-            copy.start()
-    return wait
-
-
 def early_kernel(
-    skip_ref, x_ref, b_ref, c_ref, step_ref, keep_ref, gate_hbm,
-    base_ref, carry_ref, state_out, gate_ref, *rest,
+    skip_ref, x_ref, gate_ref, b_ref, c_ref, step_ref, keep_ref, base_ref, carry_ref, state_out, *scratch
 ):
-    *scratch, state, sems = rest
-    wait = tile_copies(0, [(gate_hbm, gate_ref)], sems)
-    state[...] = jnp.zeros_like(state)
-    cut_by_cut(
+    state_out[...] = cut_by_cut(
         0, skip_ref, x_ref, gate_ref, b_ref, c_ref, step_ref, keep_ref, base_ref, carry_ref,
-        *scratch, state, wait, lambda: None,
-    )
-    state_out[...] = state[...]
+        *scratch, jnp.zeros(state_out.shape, f32), lambda: None,
+    )
 
 
 def late_kernel(
-    flag_ref, state_in, skip_ref, x_hbm, b_hbm, c_hbm, step_hbm, keep_hbm, gate_hbm,
-    base_ref, carry_ref, gate_ref, *rest,
+    flag_ref, state_in, skip_ref, x_hbm, gate_hbm, b_hbm, c_hbm, step_hbm, keep_hbm,
+    base_ref, carry_ref, *rest,
 ):
-    *scratch, state, sems, x_ref, b_ref, c_ref, step_ref, keep_ref, more_sems = rest
+    *scratch, x_ref, gate_ref, b_ref, c_ref, step_ref, keep_ref, sems = rest
+    size = x_ref.shape[0]
+    mine = pl.ds(size, size)
     copies = [
-        pltpu.make_async_copy(far, near, more_sems.at[i])
+        pltpu.make_async_copy(far, near, sems.at[i])
         for i, (far, near) in enumerate(
-            ((keep_hbm, keep_ref), (step_hbm, step_ref), (b_hbm, b_ref), (c_hbm, c_ref))
+            (
+                (keep_hbm, keep_ref),
+                (step_hbm, step_ref),
+                (c_hbm, c_ref),
+                (b_hbm, b_ref),
+                (x_hbm.at[mine], x_ref),
+                (gate_hbm.at[mine], gate_ref),
+            )
         )
     ]
     for copy in copies:
         copy.start()
-    skipped = x_ref.shape[0] // CUT
-    wait = tile_copies(skipped, [(x_hbm, x_ref), (gate_hbm, gate_ref)], sems)
-    state[...] = state_in[...]
     copies[0].wait()
     copies[1].wait()
 
-    def wait_both():
-        copies[2].wait()
-        copies[3].wait()
+    def wait_inputs():
+        for copy in copies[2:]:
+            copy.wait()
 
     cut_by_cut(
-        skipped, skip_ref, x_ref, gate_ref, b_ref, c_ref, step_ref, keep_ref,
-        base_ref, carry_ref, *scratch, state, wait, wait_both,
+        size // CUT, skip_ref, x_ref, gate_ref, b_ref, c_ref, step_ref, keep_ref,
+        base_ref, carry_ref, *scratch, state_in[...], wait_inputs,
     )
 
 
 def cut_by_cut(
     skipped, skip_ref, x_ref, gate_ref, b_ref, c_ref, step_ref, keep_ref, base_ref, carry_ref,
-    left, offset, factor, decays, starts, state, wait_tile, wait_rest,
+    left, offset, factor, decays, starts, state, wait_inputs,
 ):
     heads, tokens = step_ref.shape
     cuts = tokens // CUT
@@ -255,7 +239,7 @@
     low_lanes = jnp.where(iota((1, CUT), 1) < HEAD, 1.0, 0.0)
     only = [low_lanes.astype(bf16), (1.0 - low_lanes).astype(bf16)]
 
-    def one_cut(k, _):
+    def one_cut(k, now):
         at = pl.ds(pl.multiple_of(k * CUT, CUT), CUT)
         far = pl.ds(pl.multiple_of((skipped + k) * CUT, CUT), CUT)
         first = (skipped + k) * heads
@@ -265,7 +249,7 @@
         growths = [jnp.broadcast_to(growths[:, h : h + 1], (CUT, CUT)) for h in range(heads)]
         scores = jnp.where(causal, dot(c, b), 0.0)
         b_turned = b.astype(f32)
-        now = state[...]
+        ends = []
         high = now.astype(bf16)
         low = (now - high.astype(f32)).astype(bf16)
         earlier = dot(jnp.concatenate([c, c], axis=1), jnp.concatenate([high, low], axis=0))
@@ -294,13 +278,11 @@
             carry_ref[at, lanes] = (growth * per_channel(starts) * gate).astype(bf16)
             scaled = [b_turned * factor[pl.ds(first + 2 * pair + i, 1), :] for i in range(2)]
             both = dot(jnp.concatenate(scaled, axis=0).astype(bf16), x)
-            state[:, lanes] = per_channel(decays) * now[:, lanes] + two_heads(both[:STATE], both[STATE:])
-        return 0
-
-    wait_rest()
-    for k in range(mine):
-        wait_tile(k)
-    lax.fori_loop(0, mine, one_cut, 0, unroll=UNROLL)
+            ends.append(per_channel(decays) * now[:, lanes] + two_heads(both[:STATE], both[STATE:]))
+        return jnp.concatenate(ends, axis=1)
+
+    wait_inputs()
+    return lax.fori_loop(0, mine, one_cut, state, unroll=UNROLL)
 
 
 def gate_kernel(got_ref, c_ref, *refs):
@@ -395,34 +377,28 @@
     )
     rows = pltpu.VMEM((heads * cuts, CUT), f32)
     half = tokens // 2
-    row = pltpu.VMEM((STATE, channels), f32)
     part = shape((half, channels), bf16)
     turned = shape((STATE, tokens), bf16)
     per_head = shape((heads, tokens), f32)
     near_shapes = (turned, turned, per_head, per_head)
     local_shapes = (shape((half, channels), f32), part)
     half_wide = pltpu.VMEM((half, channels), bf16)
-    local_scratch = [
-        half_wide,
-        pltpu.VMEM((cuts // 2, 8, CUT), f32),
-        rows,
-        rows, rows, rows, row,
-    ]
-    message, x_near, *near = call(
+    local_scratch = [pltpu.VMEM((cuts // 2, 8, CUT), f32), rows, rows, rows, rows]
+    message, *near = call(
         end_state_kernel,
-        (shape((STATE, 1, channels + CUT), f32), part, *near_shapes),
-        [HBM] * 5,
-        [half_wide, rows, dma((6,))],
+        (shape((STATE, 1, channels + CUT), f32), part, part, *near_shapes),
+        [HBM] * 6,
+        [half_wide, rows, dma((7,))],
         flops=2 * tokens * STATE * channels,
-    )(x_in, b_turned, c_far, step_size, log_keep)
+    )(x_in, gate_in, b_turned, c_far, step_size, log_keep)
     got = exchange(message, SEQ)
     base_0, carry_0, state = call(
         early_kernel,
         (*local_shapes, shape((STATE, channels), f32)),
-        [SMEM] + [VMEM] * 5 + [HBM],
-        [*local_scratch, dma((1, cuts // 2))],
+        [SMEM] + [VMEM] * 6,
+        local_scratch,
         flops=int(5e9),
-    )(skip_gain, x_near, *near, gate_in)
+    )(skip_gain, *near)
     before, flag = call(
         functools.partial(scan_kernel, heads, FIRST["seq"]),
         (shape((STATE, 1, channels), f32), shape((8, CUT), f32)),
@@ -435,11 +411,11 @@
         local_shapes,
         [VMEM] * 2 + [SMEM] + [HBM] * 6,
         [
-            *local_scratch, dma((2, cuts // 2)), half_wide,
-            *(pltpu.VMEM(v.shape, v.dtype) for v in near_shapes), dma((4,)),
+            *local_scratch, half_wide, half_wide,
+            *(pltpu.VMEM(v.shape, v.dtype) for v in near_shapes), dma((6,)),
         ],
         flops=int(5e9),
-    )(flag, state, skip_gain, x_in, b_turned, c_far, step_size, log_keep, gate_in)
+    )(flag, state, skip_gain, x_in, gate_in, b_turned, c_far, step_size, log_keep)
     peers = lax.axis_size("chan")
     gated, squares = call(
         gate_kernel,

time: 52.6 us -> 52.1 us (level)
  waiting for transfers between devices: 0.18 us -> 1.47 us
  Pallas kernels: 14.7 us -> 13.7 us
  starting transfers between devices: 25.5 us -> 24.6 us
    all_to_all x2, waiting for transfers between devices: 0.18 us -> 1.47 us  [exchange(): return lax.all_to_all(v, axis, 0, 0, axis_index_groups=places, tiled=True)]
    all_to_all x2, starting transfers between devices: 25.5 us -> 24.6 us  [exchange(): return lax.all_to_all(v, axis, 0, 0, axis_index_groups=places, tiled=True)]
    pallas_call x1, Pallas kernels: 4.21 us -> 3.39 us  [per_device(): call(early_kernel, (*local_shapes, shape((STATE, channels), f32)), [SMEM]...]
  transfers between devices with their start and end apart: 2 -> 2, of which waited for: 1 -> 1; matrix products, arithmetic and copies ran while one was open for 0% -> 0% of each run, Pallas kernels for 17% -> 15%
where the time goes in v5:
time: 52.1 us; the launch traced here: 51.8 us
  starting transfers between devices  24.6 us (47%)
  Pallas kernels  13.7 us (26%)
  blocking collectives  12 us (23%)
  waiting for transfers between devices  1.47 us (3%)
    all_to_all x2, starting transfers between devices, exchange(): return lax.all_to_all(v, axis, 0, 0, axis_index_groups=places, tiled=True)  24.6 us
    all_to_all x1, blocking collectives, exchange(): return lax.all_to_all(v, axis, 0, 0, axis_index_groups=places, tiled=True)  12 us
    pallas_call x1, Pallas kernels, per_device(): call(late_kernel, local_shapes, [VMEM] * 2 + [SMEM] + [HBM] * 6, [*local_...  4.6 us
    pallas_call x1, Pallas kernels, per_device(): call(early_kernel, (*local_shapes, shape((STATE, channels), f32)), [SMEM]...  3.39 us
    pallas_call x1, Pallas kernels, per_device(): call(end_state_kernel, (shape((STATE, 1, channels + CUT), f32), part, par...  2.49 us
    all_to_all x2, waiting for transfers between devices, exchange(): return lax.all_to_all(v, axis, 0, 0, axis_index_groups=places, tiled=True)  1.47 us
    pallas_call x1, Pallas kernels, per_device(): call(norm_kernel, shape((tokens, channels), bf16), [VMEM] * 3, [pltpu.VME...  1.3 us
  transfers between devices with their start and end apart: 2, of which 1 were waited for; matrix products, arithmetic and copies ran while one was open for 0% of the time, Pallas kernels for 15%

profile of v5, /device:TPU:1, one launch (start us, length us, event | category | flops | bytes accessed | tf_op | source)
XLA Modules:
  0.0 51.8 jit_solution(17481735556681985151)
XLA Ops:
  0.0 2.5 %shard_map.82 = (f32[64,1,384]{2,1,0:T(1,128)}, bf16[1024,256]{1,0:T(8,128)(2,1)S(1)}, bf16[1024,256]{1,0:T(8,128)(2,1)S(1)}, bf16[64,2048]{1,0:T(8,128)(2,1)S(1...) custom-call(bf16[2048,256]{1,0:T(8,128)(2,1)} %x_hbm.3, ...), custom_call_target="tpu_custom_call" | custom-call | flops 67108864 | bytes 4194304 | tf_op jit(solution)/shard_map/pallas_call | solution.py:387
  2.5 15.2 %all-to-all-start = ((f32[64,1,384]{2,1,0:T(1,128)}), f32[64,1,384]{2,1,0:T(1,128)S(1)}, u32[]{:S(2)}, u32[]{:S(2)}) async-start(f32[64,1,384]{2,1,0:T(1,128)} %get-tuple-element.21), calls=%async_computation | async-start | bytes 196608 | tf_op jit(solution)/shard_map/all_to_all | solution.py:364
  17.7 3.4 %shard_map.83 = (f32[1024,256]{1,0:T(8,128)S(1)}, bf16[1024,256]{1,0:T(8,128)(2,1)S(1)}, f32[64,256]{1,0:T(8,128)S(1)}) custom-call(f32[4]{0:T(128)} %skip_ref.3, bf16[1024,256]{1,0:T(8,128)(2,1)S(1)} %get-tuple-element.22.x_ref, bf16[1024,256]{1,0:T(8,128)(2,1)S(1)} %get-tuple-element.23.gate_ref, bf16[64,2048]{1,0:T(8,128)(2,1)S(1)} %get-tuple-element.24.b_ref, ...), custom_call_target="tpu_custom_call" | custom-call | flops 5000000000 | bytes 4194304 | tf_op jit(solution)/shard_map/pallas_call | solution.py:395
  21.1 1.5 %all-to-all-done.got_ref = f32[64,1,384]{2,1,0:T(1,128)S(1)} async-done(((f32[64,1,384]{2,1,0:T(1,128)}), f32[64,1,384]{2,1,0:T(1,128)S(1)}, u32[]{:S(2)}, u32[]{:S(2)}) %all-to-all-start) | async-done | bytes 98336 | tf_op jit(solution)/shard_map/all_to_all | solution.py:364
  22.5 0.9 %shard_map.84 = (f32[64,1,256]{2,1,0:T(1,128)}, f32[8,128]{1,0:T(8,128)S(1)}) custom-call(f32[64,1,384]{2,1,0:T(1,128)S(1)} %all-to-all-done.got_ref, f32[64,256]{1,0:T(8,128)S(1)} %get-tuple-element.28._.state_in), custom_call_target="tpu_custom_call" | custom-call | flops 1000000 | bytes 4194304 | tf_op jit(solution)/shard_map/pallas_call | solution.py:402
  23.4 9.4 %all-to-all-start.1 = ((f32[64,1,256]{2,1,0:T(1,128)}), f32[64,1,256]{2,1,0:T(1,128)S(1)}, u32[]{:S(2)}, u32[]{:S(2)}) async-start(f32[64,1,256]{2,1,0:T(1,128)} %get-tuple-element.29), calls=%async_computation.1 | async-start | bytes 131072 | tf_op jit(solution)/shard_map/all_to_all | solution.py:364
  32.9 0.0 copy-start
  32.9 4.6 %shard_map.85 = (f32[1024,256]{1,0:T(8,128)S(1)}, bf16[1024,256]{1,0:T(8,128)(2,1)S(1)}) custom-call(f32[8,128]{1,0:T(8,128)S(1)} %get-tuple-element.32.flag_ref, f32[64,256]{1,0:T(8,128)S(1)} %get-tuple-element.28._.state_in, f32[4]{0:T(128)} %skip_ref.3, bf16[2048,256]{1,0:T(8,128)(2,1)} %x_hbm.3, bf16[2048,256]{1,0:T(8,128)(2,1)} %gate_hbm.3, ...), custom_call_target="tpu_custom_call" | custom-call | flops 5000000000 | bytes 4194304 | tf_op jit(solution)/shard_map/pallas_call | solution.py:409
  37.5 0.0 copy-start.1
  37.5 0.0 all-to-all-done.1.got_ref
  37.5 0.0 copy-done
  37.5 1.0 %shard_map.86 = (f32[2048,256]{1,0:T(8,128)S(1)}, f32[8,16,128]{2,1,0:T(8,128)S(1)}) custom-call(f32[64,1,256]{2,1,0:T(1,128)S(1)} %all-to-all-done.1.got_ref, bf16[64,2048]{1,0:T(8,128)(2,1)S(1)} %bitcast.5, f32[1024,256]{1,0:T(8,128)S(1)} %get-tuple-element.30.refs_0_, bf16[1024,256]{1,0:T(8,128)(2,1)S(1)} %get-tuple-element.31.refs_1_, ...), custom_call_target="tpu_custom_call" | custom-call | flops 67108864 | bytes 4194304 | tf_op jit(solution)/shard_map/pallas_call | solution.py:420
  38.5 12.0 %all_to_all.15.got_ref = f32[8,16,128]{2,1,0:T(8,128)S(1)} all-to-all(f32[8,16,128]{2,1,0:T(8,128)S(1)} %get-tuple-element.35), channel_id=1, replica_groups={{5,6,7,0,1,2,3,4},{13,14,15,8,9,10,11,12},{21,22,23,16,17,18,19,20},{29..., dimensions={0} | all-to-all | bytes 131072 | tf_op jit(solution)/shard_map/all_to_all | solution.py:364
  50.5 0.0 copy-done.1
  50.5 1.3 %shard_map.87 = bf16[2048,256]{1,0:T(8,128)(2,1)} custom-call(f32[8,16,128]{2,1,0:T(8,128)S(1)} %all_to_all.15.got_ref, f32[1,256]{1,0:T(1,128)S(1)} %bitcast.6, f32[2048,256]{1,0:T(8,128)S(1)} %get-tuple-element.36.gated_ref), custom_call_target="tpu_custom_call" | custom-call | flops 1000000 | bytes 4194304 | tf_op jit(solution)/shard_map/pallas_call | solution.py:427
Async XLA Ops:
  2.5 20.0 %all-to-all-start = ((f32[64,1,384]{2,1,0:T(1,128)}), f32[64,1,384]{2,1,0:T(1,128)S(1)}, u32[]{:S(2)}, u32[]{:S(2)}) async-start(f32[64,1,384]{2,1,0:T(1,128)} %get-tuple-element.21), calls=%async_computation | async-start | bytes 196608 | tf_op jit(solution)/shard_map/all_to_all | solution.py:364
  23.4 14.1 %all-to-all-start.1 = ((f32[64,1,256]{2,1,0:T(1,128)}), f32[64,1,256]{2,1,0:T(1,128)S(1)}, u32[]{:S(2)}, u32[]{:S(2)}) async-start(f32[64,1,256]{2,1,0:T(1,128)} %get-tuple-element.29), calls=%async_computation.1 | async-start | bytes 131072 | tf_op jit(solution)/shard_map/all_to_all | solution.py:364
  32.9 4.6 %copy-start = (bf16[2048,64]{0,1:T(8,128)(2,1)S(1)}, bf16[2048,64]{0,1:T(8,128)(2,1)}, u32[]{:S(2)}) copy-start(bf16[2048,64]{0,1:T(8,128)(2,1)} %param.11) | copy-start | bytes 786436
  37.5 13.0 %copy-start.1 = (f32[256]{0:T(256)S(1)}, f32[256]{0:T(256)}, u32[]{:S(2)}) copy-start(f32[256]{0:T(256)} %param.15) | copy-start | bytes 3076

commit v6 on v5

--- a/solution.py
+++ b/solution.py
@@ -20,9 +20,6 @@
 
 f32 = jnp.float32
 bf16 = jnp.bfloat16
-exact = functools.partial(
-    jnp.dot, precision=lax.Precision.HIGHEST, preferred_element_type=f32
-)
 
 
 def dot(a, b):
@@ -188,10 +185,10 @@
             (
                 (keep_hbm, keep_ref),
                 (step_hbm, step_ref),
-                (c_hbm, c_ref),
-                (b_hbm, b_ref),
                 (x_hbm.at[mine], x_ref),
                 (gate_hbm.at[mine], gate_ref),
+                (b_hbm.at[:, mine], b_ref.at[:, mine]),
+                (c_hbm.at[:, mine], c_ref.at[:, mine]),
             )
         )
     ]
@@ -229,7 +226,9 @@
     earlier_cut = (row % heads == col % heads) & (col // heads < row // heads)
     factor[...] = jnp.exp(after) * step
     decays[...] = jnp.exp(total)
-    starts[...] = jnp.exp(exact(jnp.where(earlier_cut, 1.0, 0.0), total))
+    mask = jnp.where(earlier_cut, 1.0, 0.0).astype(bf16)
+    before = sum(dot(mask, piece.astype(bf16)) for piece in reversed(split3(total)))
+    starts[...] = jnp.exp(before)
     offset[...] = jnp.log2(jnp.maximum(step, 1e-37)) - upto
     for k in range(mine):
         rows = upto[(skipped + k) * heads : (skipped + k + 1) * heads]

time: 52.1 us -> 52 us (level)
  no operation moved by 1% of the time
where the time goes in v6:
time: 52 us; the launch traced here: 51.7 us
  starting transfers between devices  24.6 us (47%)
  Pallas kernels  13.6 us (26%)
  blocking collectives  12 us (23%)
  waiting for transfers between devices  1.46 us (3%)
    all_to_all x2, starting transfers between devices, exchange(): return lax.all_to_all(v, axis, 0, 0, axis_index_groups=places, tiled=True)  24.6 us
    all_to_all x1, blocking collectives, exchange(): return lax.all_to_all(v, axis, 0, 0, axis_index_groups=places, tiled=True)  12 us
    pallas_call x1, Pallas kernels, per_device(): call(late_kernel, local_shapes, [VMEM] * 2 + [SMEM] + [HBM] * 6, [*local_...  4.5 us
    pallas_call x1, Pallas kernels, per_device(): call(early_kernel, (*local_shapes, shape((STATE, channels), f32)), [SMEM]...  3.4 us
    pallas_call x1, Pallas kernels, per_device(): call(end_state_kernel, (shape((STATE, 1, channels + CUT), f32), part, par...  2.49 us
    all_to_all x2, waiting for transfers between devices, exchange(): return lax.all_to_all(v, axis, 0, 0, axis_index_groups=places, tiled=True)  1.46 us
    pallas_call x1, Pallas kernels, per_device(): call(norm_kernel, shape((tokens, channels), bf16), [VMEM] * 3, [pltpu.VME...  1.3 us
  transfers between devices with their start and end apart: 2, of which 1 were waited for; matrix products, arithmetic and copies ran while one was open for 0% of the time, Pallas kernels for 15%

profile of v6, /device:TPU:1, one launch (start us, length us, event | category | flops | bytes accessed | tf_op | source)
XLA Modules:
  0.0 51.7 jit_solution(11886952130718893301)
XLA Ops:
  0.0 2.5 %shard_map.82 = (f32[64,1,384]{2,1,0:T(1,128)}, bf16[1024,256]{1,0:T(8,128)(2,1)S(1)}, bf16[1024,256]{1,0:T(8,128)(2,1)S(1)}, bf16[64,2048]{1,0:T(8,128)(2,1)S(1...) custom-call(bf16[2048,256]{1,0:T(8,128)(2,1)} %x_hbm.3, ...), custom_call_target="tpu_custom_call" | custom-call | flops 67108864 | bytes 4194304 | tf_op jit(solution)/shard_map/pallas_call | solution.py:386
  2.5 15.2 %all-to-all-start = ((f32[64,1,384]{2,1,0:T(1,128)}), f32[64,1,384]{2,1,0:T(1,128)S(1)}, u32[]{:S(2)}, u32[]{:S(2)}) async-start(f32[64,1,384]{2,1,0:T(1,128)} %get-tuple-element.21), calls=%async_computation | async-start | bytes 196608 | tf_op jit(solution)/shard_map/all_to_all | solution.py:363
  17.7 3.4 %shard_map.83 = (f32[1024,256]{1,0:T(8,128)S(1)}, bf16[1024,256]{1,0:T(8,128)(2,1)S(1)}, f32[64,256]{1,0:T(8,128)S(1)}) custom-call(f32[4]{0:T(128)} %skip_ref.3, bf16[1024,256]{1,0:T(8,128)(2,1)S(1)} %get-tuple-element.22.x_ref, bf16[1024,256]{1,0:T(8,128)(2,1)S(1)} %get-tuple-element.23.gate_ref, bf16[64,2048]{1,0:T(8,128)(2,1)S(1)} %get-tuple-element.24.b_ref, ...), custom_call_target="tpu_custom_call" | custom-call | flops 5000000000 | bytes 4194304 | tf_op jit(solution)/shard_map/pallas_call | solution.py:394
  21.1 1.5 %all-to-all-done.got_ref = f32[64,1,384]{2,1,0:T(1,128)S(1)} async-done(((f32[64,1,384]{2,1,0:T(1,128)}), f32[64,1,384]{2,1,0:T(1,128)S(1)}, u32[]{:S(2)}, u32[]{:S(2)}) %all-to-all-start) | async-done | bytes 98336 | tf_op jit(solution)/shard_map/all_to_all | solution.py:363
  22.5 0.9 %shard_map.84 = (f32[64,1,256]{2,1,0:T(1,128)}, f32[8,128]{1,0:T(8,128)S(1)}) custom-call(f32[64,1,384]{2,1,0:T(1,128)S(1)} %all-to-all-done.got_ref, f32[64,256]{1,0:T(8,128)S(1)} %get-tuple-element.28._.state_in), custom_call_target="tpu_custom_call" | custom-call | flops 1000000 | bytes 4194304 | tf_op jit(solution)/shard_map/pallas_call | solution.py:401
  23.4 9.4 %all-to-all-start.1 = ((f32[64,1,256]{2,1,0:T(1,128)}), f32[64,1,256]{2,1,0:T(1,128)S(1)}, u32[]{:S(2)}, u32[]{:S(2)}) async-start(f32[64,1,256]{2,1,0:T(1,128)} %get-tuple-element.29), calls=%async_computation.1 | async-start | bytes 131072 | tf_op jit(solution)/shard_map/all_to_all | solution.py:363
  32.9 0.0 copy-start
  32.9 4.5 %shard_map.85 = (f32[1024,256]{1,0:T(8,128)S(1)}, bf16[1024,256]{1,0:T(8,128)(2,1)S(1)}) custom-call(f32[8,128]{1,0:T(8,128)S(1)} %get-tuple-element.32.flag_ref, f32[64,256]{1,0:T(8,128)S(1)} %get-tuple-element.28._.state_in, f32[4]{0:T(128)} %skip_ref.3, bf16[2048,256]{1,0:T(8,128)(2,1)} %x_hbm.3, bf16[2048,256]{1,0:T(8,128)(2,1)} %gate_hbm.3, ...), custom_call_target="tpu_custom_call" | custom-call | flops 5000000000 | bytes 4194304 | tf_op jit(solution)/shard_map/pallas_call | solution.py:408
  37.4 0.0 copy-start.1
  37.4 0.0 all-to-all-done.1.got_ref
  37.4 0.0 copy-done
  37.4 1.0 %shard_map.86 = (f32[2048,256]{1,0:T(8,128)S(1)}, f32[8,16,128]{2,1,0:T(8,128)S(1)}) custom-call(f32[64,1,256]{2,1,0:T(1,128)S(1)} %all-to-all-done.1.got_ref, bf16[64,2048]{1,0:T(8,128)(2,1)S(1)} %bitcast.5, f32[1024,256]{1,0:T(8,128)S(1)} %get-tuple-element.30.refs_0_, bf16[1024,256]{1,0:T(8,128)(2,1)S(1)} %get-tuple-element.31.refs_1_, ...), custom_call_target="tpu_custom_call" | custom-call | flops 67108864 | bytes 4194304 | tf_op jit(solution)/shard_map/pallas_call | solution.py:419
  38.4 12.0 %all_to_all.15.got_ref = f32[8,16,128]{2,1,0:T(8,128)S(1)} all-to-all(f32[8,16,128]{2,1,0:T(8,128)S(1)} %get-tuple-element.35), channel_id=1, replica_groups={{5,6,7,0,1,2,3,4},{13,14,15,8,9,10,11,12},{21,22,23,16,17,18,19,20},{29..., dimensions={0} | all-to-all | bytes 131072 | tf_op jit(solution)/shard_map/all_to_all | solution.py:363
  50.4 0.0 copy-done.1
  50.4 1.3 %shard_map.87 = bf16[2048,256]{1,0:T(8,128)(2,1)} custom-call(f32[8,16,128]{2,1,0:T(8,128)S(1)} %all_to_all.15.got_ref, f32[1,256]{1,0:T(1,128)S(1)} %bitcast.6, f32[2048,256]{1,0:T(8,128)S(1)} %get-tuple-element.36.gated_ref), custom_call_target="tpu_custom_call" | custom-call | flops 1000000 | bytes 4194304 | tf_op jit(solution)/shard_map/pallas_call | solution.py:426
Async XLA Ops:
  2.5 20.0 %all-to-all-start = ((f32[64,1,384]{2,1,0:T(1,128)}), f32[64,1,384]{2,1,0:T(1,128)S(1)}, u32[]{:S(2)}, u32[]{:S(2)}) async-start(f32[64,1,384]{2,1,0:T(1,128)} %get-tuple-element.21), calls=%async_computation | async-start | bytes 196608 | tf_op jit(solution)/shard_map/all_to_all | solution.py:363
  23.4 14.0 %all-to-all-start.1 = ((f32[64,1,256]{2,1,0:T(1,128)}), f32[64,1,256]{2,1,0:T(1,128)S(1)}, u32[]{:S(2)}, u32[]{:S(2)}) async-start(f32[64,1,256]{2,1,0:T(1,128)} %get-tuple-element.29), calls=%async_computation.1 | async-start | bytes 131072 | tf_op jit(solution)/shard_map/all_to_all | solution.py:363
  32.9 4.5 %copy-start = (bf16[2048,64]{0,1:T(8,128)(2,1)S(1)}, bf16[2048,64]{0,1:T(8,128)(2,1)}, u32[]{:S(2)}) copy-start(bf16[2048,64]{0,1:T(8,128)(2,1)} %param.11) | copy-start | bytes 786436
  37.4 13.0 %copy-start.1 = (f32[256]{0:T(256)S(1)}, f32[256]{0:T(256)}, u32[]{:S(2)}) copy-start(f32[256]{0:T(256)} %param.15) | copy-start | bytes 3076
